TPU v7x, 128 devices: a whole 4x4x4 slice. The times are simulated.
128 devices in a mesh: gz: 4 (over z), gy: 4 (over y), gx: 8 (over x, core).
Axes of the slice: x: 4, y: 4, z: 4, core: 2. Of those that a mesh axis runs over, the one named last changes fastest.
Arguments:
- k_cell: float32 [256, 256, 256], P('gx', 'gy', 'gz')
- k_ghost: float32 [6, 256, 256], replicated
- f_rhs: float32 [256, 256, 256], P('gx', 'gy', 'gz')
- u_init: float32 [256, 256, 256], P('gx', 'gy', 'gz')
Outputs:
- output 1: float32 [256, 256, 256], P('gx', 'gy', 'gz')
- output 2: float32 [256, 256, 256], P('gx', 'gy', 'gz')
- output 3: float32 [8], replicated
All inputs are finite; a program needn't handle non-finite values.
Results may differ from a plain program's by a relative error of at most 0.001.
Values sent between devices are 32-bit elements.
A program may use at most 1 GiB of HBM per device.

v0:
```python
import jax
import jax.numpy as jnp
from jax import lax
from jax.sharding import PartitionSpec as P

CG_ITERS = 8
GRID_AXES = ('gx', 'gy', 'gz')
MESH_AXES = ('gz', 'gy', 'gx')


def neighbour_layers(grid_field, axis_dim, axis_len):
    size_here = grid_field.shape[axis_dim]
    low_layer = lax.slice_in_dim(grid_field, 0, 1, axis=axis_dim)
    top_layer = lax.slice_in_dim(grid_field, size_here - 1, size_here, axis=axis_dim)
    if axis_len == 1:
        return jnp.zeros_like(top_layer), jnp.zeros_like(low_layer)
    upward = [(src_rank, src_rank + 1) for src_rank in range(axis_len - 1)]
    downward = [(src_rank + 1, src_rank) for src_rank in range(axis_len - 1)]
    from_below = lax.ppermute(top_layer, GRID_AXES[axis_dim], upward)
    from_above = lax.ppermute(low_layer, GRID_AXES[axis_dim], downward)
    return from_below, from_above


def harmonic_faces(k_ext, axis_dim):
    size_here = k_ext.shape[axis_dim]
    left_k = lax.slice_in_dim(k_ext, 0, size_here - 1, axis=axis_dim)
    right_k = lax.slice_in_dim(k_ext, 1, size_here, axis=axis_dim)
    return 2.0 * left_k * right_k / (left_k + right_k)


def apply_operator(grid_field, face_coefs, layers):
    op_total = None
    for axis_dim in range(3):
        from_below, from_above = layers[axis_dim]
        padded = jnp.concatenate([from_below, grid_field, from_above], axis=axis_dim)
        size_here = padded.shape[axis_dim]
        face_flux = face_coefs[axis_dim] * (lax.slice_in_dim(padded, 1, size_here, axis=axis_dim) - lax.slice_in_dim(padded, 0, size_here - 1, axis=axis_dim))
        axis_part = lax.slice_in_dim(face_flux, 0, size_here - 2, axis=axis_dim) - lax.slice_in_dim(face_flux, 1, size_here - 1, axis=axis_dim)
        op_total = axis_part if op_total is None else op_total + axis_part
    return op_total


def diagonal(face_coefs):
    diag_sum = None
    for axis_dim in range(3):
        size_here = face_coefs[axis_dim].shape[axis_dim]
        low_coef = lax.slice_in_dim(face_coefs[axis_dim], 0, size_here - 1, axis=axis_dim)
        high_coef = lax.slice_in_dim(face_coefs[axis_dim], 1, size_here, axis=axis_dim)
        diag_sum = low_coef + high_coef if diag_sum is None else diag_sum + low_coef + high_coef
    return diag_sum


def local_coefs(k_cell, k_ghost, coords, counts):
    block_shape = k_cell.shape
    face_coefs = []
    for axis_dim in range(3):
        others = [other_dim for other_dim in range(3) if other_dim != axis_dim]
        starts = (coords[others[0]] * block_shape[others[0]], coords[others[1]] * block_shape[others[1]])
        extent = (block_shape[others[0]], block_shape[others[1]])
        low_wall = jnp.expand_dims(lax.dynamic_slice(k_ghost[2 * axis_dim], starts, extent), axis_dim)
        high_wall = jnp.expand_dims(lax.dynamic_slice(k_ghost[2 * axis_dim + 1], starts, extent), axis_dim)
        from_below, from_above = neighbour_layers(k_cell, axis_dim, counts[axis_dim])
        from_below = jnp.where(coords[axis_dim] == 0, low_wall, from_below)
        from_above = jnp.where(coords[axis_dim] == counts[axis_dim] - 1, high_wall, from_above)
        face_coefs.append(harmonic_faces(jnp.concatenate([from_below, k_cell, from_above], axis=axis_dim), axis_dim))
    return face_coefs


def solution(mesh):
    counts = tuple(mesh.shape[axis_name] for axis_name in GRID_AXES)
    grid_spec = P('gx', 'gy', 'gz')

    def global_sum(local_value):
        return lax.psum(local_value, MESH_AXES)

    def local_solve(k_cell, k_ghost, f_rhs, u_init):
        coords = [lax.axis_index(axis_name) for axis_name in GRID_AXES]
        face_coefs = local_coefs(k_cell, k_ghost, coords, counts)
        inv_diag = 1.0 / diagonal(face_coefs)

        def apply_stencil(grid_field):
            layers = [neighbour_layers(grid_field, axis_dim, counts[axis_dim]) for axis_dim in range(3)]
            return apply_operator(grid_field, face_coefs, layers)

        residual = f_rhs - apply_stencil(u_init)
        precond = residual * inv_diag
        rz_old = global_sum(jnp.sum(residual * precond))
        approx = u_init
        direction = precond
        history = []
        for iteration in range(CG_ITERS):
            q_vec = apply_stencil(direction)
            step_alpha = rz_old / global_sum(jnp.sum(direction * q_vec))
            approx = approx + step_alpha * direction
            residual = residual - step_alpha * q_vec
            precond = residual * inv_diag
            pair_sums = global_sum(jnp.stack([jnp.sum(residual * precond), jnp.sum(residual * residual)]))
            direction = precond + (pair_sums[0] / rz_old) * direction
            rz_old = pair_sums[0]
            history.append(pair_sums[1])
        return approx, residual, jnp.stack(history)

    return jax.shard_map(local_solve, mesh=mesh, in_specs=(grid_spec, P(), grid_spec, grid_spec), out_specs=(grid_spec, grid_spec, P()), check_vma=False)
```

profile of v0, /device:TPU:0, one launch (start us, length us, event | category | flops | bytes accessed | tf_op | source)
XLA Modules:
  0.0 1445.3 jit_solution(11937949739165816467)
XLA Ops:
  5.8 5.2 collective-permute-start.11
  16.9 5.3 collective-permute-start.8
  29.8 5.1 collective-permute-start.7
  37.1 4.2 collective-permute-done.5
  60.5 3.9 collective-permute-start
  79.5 4.5 collective-permute-start.17
  85.4 4.8 collective-permute-start.15
  92.6 3.6 collective-permute-start.13
  106.6 67.3 %all-reduce = (f32[]{:T(128)}, f32[]{:T(128)}) all-reduce(f32[]{:T(128)} %get-tuple-element.29, f32[]{:T(128)} %get-tuple-element.28), channel_id=1, replica_groups=mesh['gz'=4,'gy'=4,'gx'=8] {'gz','gy','gx'}, use_global_device_ids=true, to_apply=%region_1.2 | all-reduce | flops 2 | bytes 16 | tf_op jit(solution)/shard_map/psum | solution.py:74
  175.2 4.0 multiply_reduce_fusion.21
  180.5 63.6 %psum.121 = f32[2]{0:T(128)S(1)} all-reduce(f32[2]{0:T(128)S(1)} %pad_maximum_fusion.6), channel_id=1, replica_groups=mesh['gz'=4,'gy'=4,'gx'=8] {'gz','gy','gx'}, use_global_device_ids=true, to_apply=%region_6.7 | all-reduce | flops 2 | bytes 16 | tf_op jit(solution)/shard_map/psum | solution.py:74
  254.1 4.5 collective-permute-start.23
  259.9 4.5 collective-permute-start.21
  279.0 63.1 %psum.122 = f32[]{:T(128)} all-reduce(f32[]{:T(128)} %get-tuple-element.57), channel_id=1, replica_groups=mesh['gz'=4,'gy'=4,'gx'=8] {'gz','gy','gx'}, use_global_device_ids=true, to_apply=%region_8.9 | all-reduce | flops 1 | bytes 8 | tf_op jit(solution)/shard_map/psum | solution.py:74
  343.4 4.2 multiply_reduce_fusion.18
  348.9 64.0 %psum.123 = f32[2]{0:T(128)S(1)} all-reduce(f32[2]{0:T(128)S(1)} %pad_maximum_fusion.7), channel_id=1, replica_groups=mesh['gz'=4,'gy'=4,'gx'=8] {'gz','gy','gx'}, use_global_device_ids=true, to_apply=%region_11.12 | all-reduce | flops 2 | bytes 16 | tf_op jit(solution)/shard_map/psum | solution.py:74
  422.9 4.5 collective-permute-start.29
  428.7 4.5 collective-permute-start.27
  449.8 62.3 %psum.124 = f32[]{:T(128)} all-reduce(f32[]{:T(128)} %get-tuple-element.53), channel_id=1, replica_groups=mesh['gz'=4,'gy'=4,'gx'=8] {'gz','gy','gx'}, use_global_device_ids=true, to_apply=%region_13.14 | all-reduce | flops 1 | bytes 8 | tf_op jit(solution)/shard_map/psum | solution.py:74
  513.4 4.2 multiply_reduce_fusion.15
  518.9 63.9 %psum.125 = f32[2]{0:T(128)S(1)} all-reduce(f32[2]{0:T(128)S(1)} %pad_maximum_fusion.8), channel_id=1, replica_groups=mesh['gz'=4,'gy'=4,'gx'=8] {'gz','gy','gx'}, use_global_device_ids=true, to_apply=%region_16.17 | all-reduce | flops 2 | bytes 16 | tf_op jit(solution)/shard_map/psum | solution.py:74
  593.1 4.5 collective-permute-start.35
  598.9 4.5 collective-permute-start.33
  620.0 62.3 %psum.126 = f32[]{:T(128)} all-reduce(f32[]{:T(128)} %get-tuple-element.49), channel_id=1, replica_groups=mesh['gz'=4,'gy'=4,'gx'=8] {'gz','gy','gx'}, use_global_device_ids=true, to_apply=%region_18.19 | all-reduce | flops 1 | bytes 8 | tf_op jit(solution)/shard_map/psum | solution.py:74
  683.6 4.2 multiply_reduce_fusion.12
  689.1 64.0 %psum.127 = f32[2]{0:T(128)S(1)} all-reduce(f32[2]{0:T(128)S(1)} %pad_maximum_fusion.9), channel_id=1, replica_groups=mesh['gz'=4,'gy'=4,'gx'=8] {'gz','gy','gx'}, use_global_device_ids=true, to_apply=%region_21.22 | all-reduce | flops 2 | bytes 16 | tf_op jit(solution)/shard_map/psum | solution.py:74
  763.2 4.5 collective-permute-start.41
  769.1 4.5 collective-permute-start.39
  776.0 3.2 collective-permute-start.37
  790.4 62.3 %psum.128 = f32[]{:T(128)} all-reduce(f32[]{:T(128)} %get-tuple-element.45), channel_id=1, replica_groups=mesh['gz'=4,'gy'=4,'gx'=8] {'gz','gy','gx'}, use_global_device_ids=true, to_apply=%region_23.24 | all-reduce | flops 1 | bytes 8 | tf_op jit(solution)/shard_map/psum | solution.py:74
  853.9 4.2 multiply_reduce_fusion.9
  859.4 63.7 %psum.129 = f32[2]{0:T(128)S(1)} all-reduce(f32[2]{0:T(128)S(1)} %pad_maximum_fusion.10), channel_id=1, replica_groups=mesh['gz'=4,'gy'=4,'gx'=8] {'gz','gy','gx'}, use_global_device_ids=true, to_apply=%region_26.27 | all-reduce | flops 2 | bytes 16 | tf_op jit(solution)/shard_map/psum | solution.py:74
  933.4 4.5 collective-permute-start.47
  939.2 4.5 collective-permute-start.45
  960.4 62.8 %psum.130 = f32[]{:T(128)} all-reduce(f32[]{:T(128)} %get-tuple-element.41), channel_id=1, replica_groups=mesh['gz'=4,'gy'=4,'gx'=8] {'gz','gy','gx'}, use_global_device_ids=true, to_apply=%region_28.29 | all-reduce | flops 1 | bytes 8 | tf_op jit(solution)/shard_map/psum | solution.py:74
  1024.4 4.3 multiply_reduce_fusion.6
  1030.0 64.0 %psum.131 = f32[2]{0:T(128)S(1)} all-reduce(f32[2]{0:T(128)S(1)} %pad_maximum_fusion.11), channel_id=1, replica_groups=mesh['gz'=4,'gy'=4,'gx'=8] {'gz','gy','gx'}, use_global_device_ids=true, to_apply=%region_31.32 | all-reduce | flops 2 | bytes 16 | tf_op jit(solution)/shard_map/psum | solution.py:74
  1104.3 4.5 collective-permute-start.53
  1110.2 4.5 collective-permute-start.51
  1131.2 62.3 %psum.132 = f32[]{:T(128)} all-reduce(f32[]{:T(128)} %get-tuple-element.37), channel_id=1, replica_groups=mesh['gz'=4,'gy'=4,'gx'=8] {'gz','gy','gx'}, use_global_device_ids=true, to_apply=%region_33.34 | all-reduce | flops 1 | bytes 8 | tf_op jit(solution)/shard_map/psum | solution.py:74
  1194.8 4.2 multiply_reduce_fusion.3
  1200.4 63.9 %psum.133 = f32[2]{0:T(128)S(1)} all-reduce(f32[2]{0:T(128)S(1)} %pad_maximum_fusion.12), channel_id=1, replica_groups=mesh['gz'=4,'gy'=4,'gx'=8] {'gz','gy','gx'}, use_global_device_ids=true, to_apply=%region_36.37 | all-reduce | flops 2 | bytes 16 | tf_op jit(solution)/shard_map/psum | solution.py:74
  1274.6 4.5 collective-permute-start.59
  1280.4 4.5 collective-permute-start.57
  1301.5 62.3 %psum.134 = f32[]{:T(128)} all-reduce(f32[]{:T(128)} %get-tuple-element.33), channel_id=1, replica_groups=mesh['gz'=4,'gy'=4,'gx'=8] {'gz','gy','gx'}, use_global_device_ids=true, to_apply=%region_38.39 | all-reduce | flops 1 | bytes 8 | tf_op jit(solution)/shard_map/psum | solution.py:74
  1365.1 4.1 multiply_add_fusion
  1375.0 64.0 %psum.135 = f32[2]{0:T(128)S(1)} all-reduce(f32[2]{0:T(128)S(1)} %pad_maximum_fusion.13), channel_id=1, replica_groups=mesh['gz'=4,'gy'=4,'gx'=8] {'gz','gy','gx'}, use_global_device_ids=true, to_apply=%region_41.42 | all-reduce | flops 2 | bytes 16 | tf_op jit(solution)/shard_map/psum | solution.py:74
  1439.6 5.6 stack.99
  (340 shorter events, 265.2 us)
Async XLA Ops:
  3.6 47.4 %collective-permute-start.10 = (f32[32,64,1]{1,0,2:T(8,128)}, f32[32,64,1]{1,0,2:T(8,128)}, u32[]{:S(2)}, u32[]{:S(2)}) collective-permute-start(f32[32,64,1]{1,0,2:T(8,128)} %copy.145), channel_id=1, source_target_pairs={{32,0},{64,32},{96,64},{33,1},{65,33},{97,65},{34,2},{66,34},{98,6... | collective-permute-start | bytes 24584 | tf_op jit(solution)/shard_map/ppermute | solution.py:20
  5.8 50.8 %collective-permute-start.11 = (f32[32,64,1]{1,0,2:T(8,128)}, f32[32,64,1]{1,0,2:T(8,128)}, u32[]{:S(2)}, u32[]{:S(2)}) collective-permute-start(f32[32,64,1]{1,0,2:T(8,128)} %copy.146), channel_id=1, source_target_pairs={{0,32},{32,64},{64,96},{1,33},{33,65},{65,97},{2,34},{34,66},{66,9... | collective-permute-start | bytes 24584 | tf_op jit(solution)/shard_map/ppermute | solution.py:19
  14.6 15.1 %collective-permute-start.9 = (f32[32,64,1]{1,0,2:T(8,128)}, f32[32,64,1]{1,0,2:T(8,128)}, u32[]{:S(2)}, u32[]{:S(2)}) collective-permute-start(f32[32,64,1]{1,0,2:T(8,128)} %copy.144), channel_id=1, source_target_pairs={{32,0},{64,32},{96,64},{33,1},{65,33},{97,65},{34,2},{66,34},{98,6... | collective-permute-start | bytes 24584 | tf_op jit(solution)/shard_map/ppermute | solution.py:20
  16.9 18.8 %collective-permute-start.8 = (f32[32,64,1]{1,0,2:T(8,128)}, f32[32,64,1]{1,0,2:T(8,128)}, u32[]{:S(2)}, u32[]{:S(2)}) collective-permute-start(f32[32,64,1]{1,0,2:T(8,128)} %copy.143), channel_id=1, source_target_pairs={{0,32},{32,64},{64,96},{1,33},{33,65},{65,97},{2,34},{34,66},{66,9... | collective-permute-start | bytes 24584 | tf_op jit(solution)/shard_map/ppermute | solution.py:19
  23.4 37.0 %collective-permute-start.6 = (f32[32,1,64]{2,0,1:T(8,128)}, f32[32,1,64]{2,0,1:T(8,128)}, u32[]{:S(2)}, u32[]{:S(2)}) collective-permute-start(f32[32,1,64]{2,0,1:T(8,128)} %get-tuple-element.132), channel_id=1, source_target_pairs={{8,0},{16,8},{24,16},{9,1},{17,9},{25,17},{10,2},{18,10},{26,18},{... | collective-permute-start | bytes 24584 | tf_op jit(solution)/shard_map/ppermute | solution.py:20
  29.8 34.6 %collective-permute-start.7 = (f32[32,1,64]{2,0,1:T(8,128)}, f32[32,1,64]{2,0,1:T(8,128)}, u32[]{:S(2)}, u32[]{:S(2)}) collective-permute-start(f32[32,1,64]{2,0,1:T(8,128)} %get-tuple-element.131), channel_id=1, source_target_pairs={{0,8},{8,16},{16,24},{1,9},{9,17},{17,25},{2,10},{10,18},{18,26},{... | collective-permute-start | bytes 24584 | tf_op jit(solution)/shard_map/ppermute | solution.py:19
  45.9 22.8 %collective-permute-start.2 = (f32[1,64,64]{2,0,1:T(1,128)S(1)}, f32[1,64,64]{2,0,1:T(1,128)S(1)}, u32[]{:S(2)}, u32[]{:S(2)}) collective-permute-start(f32[1,64,64]{2,0,1:T(1,128)S(1)} %bitcast.66), channel_id=1, source_target_pairs={{1,0},{2,1},{3,2},{4,3},{5,4},{6,5},{7,6},{9,8},{10,9},{11,10},{12... | collective-permute-start | bytes 49160 | tf_op jit(solution)/shard_map/ppermute | solution.py:20
  50.9 17.8 %collective-permute-start.3 = (f32[1,64,64]{2,0,1:T(1,128)S(1)}, f32[1,64,64]{2,0,1:T(1,128)S(1)}, u32[]{:S(2)}, u32[]{:S(2)}) collective-permute-start(f32[1,64,64]{2,0,1:T(1,128)S(1)} %bitcast.65), channel_id=1, source_target_pairs={{0,1},{1,2},{2,3},{3,4},{4,5},{5,6},{6,7},{8,9},{9,10},{10,11},{11... | collective-permute-start | bytes 49160 | tf_op jit(solution)/shard_map/ppermute | solution.py:19
  56.6 12.0 collective-permute-start.1
  76.5 16.1 %collective-permute-start.16 = (f32[32,64,1]{1,0,2:T(8,128)S(1)}, f32[32,64,1]{1,0,2:T(8,128)S(1)}, u32[]{:S(2)}, u32[]{:S(2)}) collective-permute-start(f32[32,64,1]{1,0,2:T(8,128)S(1)} %copy.106), channel_id=1, source_target_pairs={{32,0},{64,32},{96,64},{33,1},{65,33},{97,65},{34,2},{66,34},{98,6... | collective-permute-start | bytes 24584 | tf_op jit(solution)/shard_map/ppermute | solution.py:20
  79.5 18.5 %collective-permute-start.17 = (f32[32,64,1]{1,0,2:T(8,128)S(1)}, f32[32,64,1]{1,0,2:T(8,128)S(1)}, u32[]{:S(2)}, u32[]{:S(2)}) collective-permute-start(f32[32,64,1]{1,0,2:T(8,128)S(1)} %copy.108), channel_id=1, source_target_pairs={{0,32},{32,64},{64,96},{1,33},{33,65},{65,97},{2,34},{34,66},{66,9... | collective-permute-start | bytes 24584 | tf_op jit(solution)/shard_map/ppermute | solution.py:19
  84.1 15.8 %collective-permute-start.14 = (f32[32,1,64]{2,0,1:T(8,128)S(1)}, f32[32,1,64]{2,0,1:T(8,128)S(1)}, u32[]{:S(2)}, u32[]{:S(2)}) collective-permute-start(f32[32,1,64]{2,0,1:T(8,128)S(1)} %get-tuple-element.122), channel_id=1, source_target_pairs={{8,0},{16,8},{24,16},{9,1},{17,9},{25,17},{10,2},{18,10},{26,18},{... | collective-permute-start | bytes 24584 | tf_op jit(solution)/shard_map/ppermute | solution.py:20
  85.4 14.6 %collective-permute-start.15 = (f32[32,1,64]{2,0,1:T(8,128)S(1)}, f32[32,1,64]{2,0,1:T(8,128)S(1)}, u32[]{:S(2)}, u32[]{:S(2)}) collective-permute-start(f32[32,1,64]{2,0,1:T(8,128)S(1)} %get-tuple-element.121), channel_id=1, source_target_pairs={{0,8},{8,16},{16,24},{1,9},{9,17},{17,25},{2,10},{10,18},{18,26},{... | collective-permute-start | bytes 24584 | tf_op jit(solution)/shard_map/ppermute | solution.py:19
  91.3 11.8 collective-permute-start.12
  251.0 14.8 %collective-permute-start.22 = (f32[32,64,1]{1,0,2:T(8,128)S(1)}, f32[32,64,1]{1,0,2:T(8,128)S(1)}, u32[]{:S(2)}, u32[]{:S(2)}) collective-permute-start(f32[32,64,1]{1,0,2:T(8,128)S(1)} %copy.111), channel_id=1, source_target_pairs={{32,0},{64,32},{96,64},{33,1},{65,33},{97,65},{34,2},{66,34},{98,6... | collective-permute-start | bytes 24584 | tf_op jit(solution)/shard_map/ppermute | solution.py:20
  254.1 16.6 %collective-permute-start.23 = (f32[32,64,1]{1,0,2:T(8,128)S(1)}, f32[32,64,1]{1,0,2:T(8,128)S(1)}, u32[]{:S(2)}, u32[]{:S(2)}) collective-permute-start(f32[32,64,1]{1,0,2:T(8,128)S(1)} %copy.113), channel_id=1, source_target_pairs={{0,32},{32,64},{64,96},{1,33},{33,65},{65,97},{2,34},{34,66},{66,9... | collective-permute-start | bytes 24584 | tf_op jit(solution)/shard_map/ppermute | solution.py:19
  258.6 13.9 collective-permute-start.20
  259.9 12.6 collective-permute-start.21
  419.8 15.9 %collective-permute-start.28 = (f32[32,64,1]{1,0,2:T(8,128)S(1)}, f32[32,64,1]{1,0,2:T(8,128)S(1)}, u32[]{:S(2)}, u32[]{:S(2)}) collective-permute-start(f32[32,64,1]{1,0,2:T(8,128)S(1)} %copy.115), channel_id=1, source_target_pairs={{32,0},{64,32},{96,64},{33,1},{65,33},{97,65},{34,2},{66,34},{98,6... | collective-permute-start | bytes 24584 | tf_op jit(solution)/shard_map/ppermute | solution.py:20
  422.9 17.7 %collective-permute-start.29 = (f32[32,64,1]{1,0,2:T(8,128)S(1)}, f32[32,64,1]{1,0,2:T(8,128)S(1)}, u32[]{:S(2)}, u32[]{:S(2)}) collective-permute-start(f32[32,64,1]{1,0,2:T(8,128)S(1)} %copy.117), channel_id=1, source_target_pairs={{0,32},{32,64},{64,96},{1,33},{33,65},{65,97},{2,34},{34,66},{66,9... | collective-permute-start | bytes 24584 | tf_op jit(solution)/shard_map/ppermute | solution.py:19
  427.4 15.0 %collective-permute-start.26 = (f32[32,1,64]{2,0,1:T(8,128)S(1)}, f32[32,1,64]{2,0,1:T(8,128)S(1)}, u32[]{:S(2)}, u32[]{:S(2)}) collective-permute-start(f32[32,1,64]{2,0,1:T(8,128)S(1)} %get-tuple-element.110), channel_id=1, source_target_pairs={{8,0},{16,8},{24,16},{9,1},{17,9},{25,17},{10,2},{18,10},{26,18},{... | collective-permute-start | bytes 24584 | tf_op jit(solution)/shard_map/ppermute | solution.py:20
  428.7 13.7 collective-permute-start.27
  434.4 12.7 collective-permute-start.24
  590.0 15.9 %collective-permute-start.34 = (f32[32,64,1]{1,0,2:T(8,128)S(1)}, f32[32,64,1]{1,0,2:T(8,128)S(1)}, u32[]{:S(2)}, u32[]{:S(2)}) collective-permute-start(f32[32,64,1]{1,0,2:T(8,128)S(1)} %copy.119), channel_id=1, source_target_pairs={{32,0},{64,32},{96,64},{33,1},{65,33},{97,65},{34,2},{66,34},{98,6... | collective-permute-start | bytes 24584 | tf_op jit(solution)/shard_map/ppermute | solution.py:20
  593.1 17.7 %collective-permute-start.35 = (f32[32,64,1]{1,0,2:T(8,128)S(1)}, f32[32,64,1]{1,0,2:T(8,128)S(1)}, u32[]{:S(2)}, u32[]{:S(2)}) collective-permute-start(f32[32,64,1]{1,0,2:T(8,128)S(1)} %copy.121), channel_id=1, source_target_pairs={{0,32},{32,64},{64,96},{1,33},{33,65},{65,97},{2,34},{34,66},{66,9... | collective-permute-start | bytes 24584 | tf_op jit(solution)/shard_map/ppermute | solution.py:19
  597.6 14.9 %collective-permute-start.32 = (f32[32,1,64]{2,0,1:T(8,128)S(1)}, f32[32,1,64]{2,0,1:T(8,128)S(1)}, u32[]{:S(2)}, u32[]{:S(2)}) collective-permute-start(f32[32,1,64]{2,0,1:T(8,128)S(1)} %get-tuple-element.104), channel_id=1, source_target_pairs={{8,0},{16,8},{24,16},{9,1},{17,9},{25,17},{10,2},{18,10},{26,18},{... | collective-permute-start | bytes 24584 | tf_op jit(solution)/shard_map/ppermute | solution.py:20
  598.9 13.7 collective-permute-start.33
  604.5 12.7 collective-permute-start.30
  760.2 15.9 %collective-permute-start.40 = (f32[32,64,1]{1,0,2:T(8,128)S(1)}, f32[32,64,1]{1,0,2:T(8,128)S(1)}, u32[]{:S(2)}, u32[]{:S(2)}) collective-permute-start(f32[32,64,1]{1,0,2:T(8,128)S(1)} %copy.123), channel_id=1, source_target_pairs={{32,0},{64,32},{96,64},{33,1},{65,33},{97,65},{34,2},{66,34},{98,6... | collective-permute-start | bytes 24584 | tf_op jit(solution)/shard_map/ppermute | solution.py:20
  763.2 17.9 %collective-permute-start.41 = (f32[32,64,1]{1,0,2:T(8,128)S(1)}, f32[32,64,1]{1,0,2:T(8,128)S(1)}, u32[]{:S(2)}, u32[]{:S(2)}) collective-permute-start(f32[32,64,1]{1,0,2:T(8,128)S(1)} %copy.125), channel_id=1, source_target_pairs={{0,32},{32,64},{64,96},{1,33},{33,65},{65,97},{2,34},{34,66},{66,9... | collective-permute-start | bytes 24584 | tf_op jit(solution)/shard_map/ppermute | solution.py:19
  767.8 15.1 %collective-permute-start.38 = (f32[32,1,64]{2,0,1:T(8,128)S(1)}, f32[32,1,64]{2,0,1:T(8,128)S(1)}, u32[]{:S(2)}, u32[]{:S(2)}) collective-permute-start(f32[32,1,64]{2,0,1:T(8,128)S(1)} %get-tuple-element.98), channel_id=1, source_target_pairs={{8,0},{16,8},{24,16},{9,1},{17,9},{25,17},{10,2},{18,10},{26,18},{... | collective-permute-start | bytes 24584 | tf_op jit(solution)/shard_map/ppermute | solution.py:20
  769.1 13.8 collective-permute-start.39
  774.7 12.8 collective-permute-start.36
  930.3 15.9 %collective-permute-start.46 = (f32[32,64,1]{1,0,2:T(8,128)S(1)}, f32[32,64,1]{1,0,2:T(8,128)S(1)}, u32[]{:S(2)}, u32[]{:S(2)}) collective-permute-start(f32[32,64,1]{1,0,2:T(8,128)S(1)} %copy.127), channel_id=1, source_target_pairs={{32,0},{64,32},{96,64},{33,1},{65,33},{97,65},{34,2},{66,34},{98,6... | collective-permute-start | bytes 24584 | tf_op jit(solution)/shard_map/ppermute | solution.py:20
  933.4 17.6 %collective-permute-start.47 = (f32[32,64,1]{1,0,2:T(8,128)S(1)}, f32[32,64,1]{1,0,2:T(8,128)S(1)}, u32[]{:S(2)}, u32[]{:S(2)}) collective-permute-start(f32[32,64,1]{1,0,2:T(8,128)S(1)} %copy.129), channel_id=1, source_target_pairs={{0,32},{32,64},{64,96},{1,33},{33,65},{65,97},{2,34},{34,66},{66,9... | collective-permute-start | bytes 24584 | tf_op jit(solution)/shard_map/ppermute | solution.py:19
  937.9 15.0 %collective-permute-start.44 = (f32[32,1,64]{2,0,1:T(8,128)S(1)}, f32[32,1,64]{2,0,1:T(8,128)S(1)}, u32[]{:S(2)}, u32[]{:S(2)}) collective-permute-start(f32[32,1,64]{2,0,1:T(8,128)S(1)} %get-tuple-element.92), channel_id=1, source_target_pairs={{8,0},{16,8},{24,16},{9,1},{17,9},{25,17},{10,2},{18,10},{26,18},{... | collective-permute-start | bytes 24584 | tf_op jit(solution)/shard_map/ppermute | solution.py:20
  939.2 13.7 collective-permute-start.45
  944.9 12.7 collective-permute-start.42
  1101.3 15.9 %collective-permute-start.52 = (f32[32,64,1]{1,0,2:T(8,128)S(1)}, f32[32,64,1]{1,0,2:T(8,128)S(1)}, u32[]{:S(2)}, u32[]{:S(2)}) collective-permute-start(f32[32,64,1]{1,0,2:T(8,128)S(1)} %copy.131), channel_id=1, source_target_pairs={{32,0},{64,32},{96,64},{33,1},{65,33},{97,65},{34,2},{66,34},{98,6... | collective-permute-start | bytes 24584 | tf_op jit(solution)/shard_map/ppermute | solution.py:20
  1104.3 17.6 %collective-permute-start.53 = (f32[32,64,1]{1,0,2:T(8,128)S(1)}, f32[32,64,1]{1,0,2:T(8,128)S(1)}, u32[]{:S(2)}, u32[]{:S(2)}) collective-permute-start(f32[32,64,1]{1,0,2:T(8,128)S(1)} %copy.133), channel_id=1, source_target_pairs={{0,32},{32,64},{64,96},{1,33},{33,65},{65,97},{2,34},{34,66},{66,9... | collective-permute-start | bytes 24584 | tf_op jit(solution)/shard_map/ppermute | solution.py:19
  1108.9 14.9 %collective-permute-start.50 = (f32[32,1,64]{2,0,1:T(8,128)S(1)}, f32[32,1,64]{2,0,1:T(8,128)S(1)}, u32[]{:S(2)}, u32[]{:S(2)}) collective-permute-start(f32[32,1,64]{2,0,1:T(8,128)S(1)} %get-tuple-element.86), channel_id=1, source_target_pairs={{8,0},{16,8},{24,16},{9,1},{17,9},{25,17},{10,2},{18,10},{26,18},{... | collective-permute-start | bytes 24584 | tf_op jit(solution)/shard_map/ppermute | solution.py:20
  1110.2 13.6 collective-permute-start.51
  1115.8 12.6 collective-permute-start.48
  1271.5 15.9 %collective-permute-start.58 = (f32[32,64,1]{1,0,2:T(8,128)S(1)}, f32[32,64,1]{1,0,2:T(8,128)S(1)}, u32[]{:S(2)}, u32[]{:S(2)}) collective-permute-start(f32[32,64,1]{1,0,2:T(8,128)S(1)} %copy.135), channel_id=1, source_target_pairs={{32,0},{64,32},{96,64},{33,1},{65,33},{97,65},{34,2},{66,34},{98,6... | collective-permute-start | bytes 24584 | tf_op jit(solution)/shard_map/ppermute | solution.py:20
  1274.6 17.6 %collective-permute-start.59 = (f32[32,64,1]{1,0,2:T(8,128)S(1)}, f32[32,64,1]{1,0,2:T(8,128)S(1)}, u32[]{:S(2)}, u32[]{:S(2)}) collective-permute-start(f32[32,64,1]{1,0,2:T(8,128)S(1)} %copy.137), channel_id=1, source_target_pairs={{0,32},{32,64},{64,96},{1,33},{33,65},{65,97},{2,34},{34,66},{66,9... | collective-permute-start | bytes 24584 | tf_op jit(solution)/shard_map/ppermute | solution.py:19
  1279.1 14.9 %collective-permute-start.56 = (f32[32,1,64]{2,0,1:T(8,128)S(1)}, f32[32,1,64]{2,0,1:T(8,128)S(1)}, u32[]{:S(2)}, u32[]{:S(2)}) collective-permute-start(f32[32,1,64]{2,0,1:T(8,128)S(1)} %get-tuple-element.80), channel_id=1, source_target_pairs={{8,0},{16,8},{24,16},{9,1},{17,9},{25,17},{10,2},{18,10},{26,18},{... | collective-permute-start | bytes 24584 | tf_op jit(solution)/shard_map/ppermute | solution.py:20
  1280.4 13.6 collective-permute-start.57
  1286.1 12.6 collective-permute-start.54
  (62 other events, 512.0 us)
where the time goes:
time: 1460 us; the launch traced here: 1450 us
  blocking collectives  1020 us (70%)
  starting transfers between devices  162 us (11%)
  local copies, waits for them, and re-layouts  120 us (8%)
  other arithmetic  119 us (8%)
  between operations  21.8 us (1%)
    psum x16, blocking collectives, global_sum(): return lax.psum(local_value, MESH_AXES)  1020 us
    ppermute x30, starting transfers between devices, neighbour_layers(): from_below = lax.ppermute(top_layer, GRID_AXES[axis_dim], upward)  124 us
    mul x27, other arithmetic, apply_operator(): face_coefs[axis_dim]  41.5 us
    slice x38, local copies, waits for them, and re-layouts, neighbour_layers(): lax.slice_in_dim(grid_field, size_here - 1, size_here, axis=axis_dim)  41.4 us
    ppermute x30, starting transfers between devices, neighbour_layers(): from_above = lax.ppermute(low_layer, GRID_AXES[axis_dim], downward)  38.6 us
    reduce_sum x8, other arithmetic, local_solve(): jnp.sum(residual * precond)  30.5 us
  transfers between devices with their start and end apart: 60, of which 2 were waited for; matrix products, arithmetic and copies ran while one was open for 7% of the time, Pallas kernels for 0%

commit v1 on v0

v1 whole, which is shorter than its diff:
```python
import functools

import jax
import jax.numpy as jnp
from jax import lax
from jax.experimental import pallas as pl
from jax.experimental.pallas import tpu as pltpu
from jax.sharding import PartitionSpec as P

CG_ITERS = 8
NB = CG_ITERS + 1
NX, NY, NZ = 32, 64, 64
NP = NX // 2
R0 = 8
MESH = pl.DeviceIdType.MESH
AXES = ('gx', 'gy', 'gz')
BOUND = 4096.0
F32 = jnp.float32
SUB, LANES, HALF, LOW = 8, 128, 64, 63
ROWS = NY // SUB
TILE = (SUB, LANES)
WIDE = (2 * SUB, LANES)
FACES = 6


def own(t):
    return slice(R0 + SUB * t, R0 + SUB * t + SUB)


def tile(t):
    return slice(SUB * t, SUB * t + SUB)


def one(i):
    return slice(i, i + 1)


def spin(values, by):
    return pltpu.roll(values, by, 1)


def turn_half(values):
    return spin(values, HALF)


def row_sum(values):
    return jnp.sum(values, axis=0, keepdims=True)


def lane_sum(values):
    return jnp.sum(values, axis=1, keepdims=True)


def total_of(parts):
    parts = list(parts)
    while len(parts) > 1:
        parts = [sum(parts[i + 1:i + 2], parts[i]) for i in range(0, len(parts), 2)]
    return parts[0]


def lane_iota(rows=8):
    return lax.broadcasted_iota(jnp.int32, (rows, LANES), 1)


def row_iota(rows):
    return lax.broadcasted_iota(jnp.int32, (rows, LANES), 0)


class Comm:
    def __init__(self, counts, bufs):
        self.counts = counts
        self.pos = [lax.axis_index(name) for name in AXES]
        self.has = []
        for axis in range(3):
            self.has.append(self.pos[axis] > 0)
            self.has.append(self.pos[axis] < counts[axis] - 1)
        (self.xs, self.ys, self.zs, self.xr, self.yr, self.zr, self.send_sem, self.recv_sem) = bufs

    def copies(self, rnd, face):
        axis, high = face // 2, face % 2
        src = (self.xs, self.ys, self.zs)[axis]
        dst = (self.xr, self.yr, self.zr)[axis]
        step = 1 if high else -1
        return pltpu.make_async_remote_copy(
            src_ref=src.at[rnd, high], dst_ref=dst.at[rnd, 1 - high],
            send_sem=self.send_sem.at[rnd, face], recv_sem=self.recv_sem.at[rnd, face ^ 1],
            device_id={AXES[axis]: self.pos[axis] + step}, device_id_type=MESH)

    def send(self, rnd, face):
        @pl.when(self.has[face])
        def _():
            self.copies(rnd, face).start()

    def wait_recv(self, rnd, face):
        axis, high = face // 2, face % 2
        src = (self.xs, self.ys, self.zs)[axis]
        dst = (self.xr, self.yr, self.zr)[axis]
        step = 1 if high else -1

        @pl.when(self.has[face])
        def _():
            pltpu.make_async_remote_copy(
                src_ref=src.at[rnd, high], dst_ref=dst.at[rnd, high],
                send_sem=self.send_sem.at[rnd, face], recv_sem=self.recv_sem.at[rnd, face],
                device_id={AXES[axis]: self.pos[axis] + step}, device_id_type=MESH).wait_recv()

    def wait_send(self, rnd, face):
        @pl.when(self.has[face])
        def _():
            self.copies(rnd, face).wait_send()


def barrier_all_lines(comm):
    sem = pltpu.get_barrier_semaphore()
    total = 0
    for axis in range(3):
        n = comm.counts[axis]
        for off in range(1, n):
            pl.semaphore_signal(sem, inc=1, device_id={AXES[axis]: lax.rem(comm.pos[axis] + off, n)}, device_id_type=MESH)
            total += 1
    return sem, total


class Reducer:
    def __init__(self, comm, send_row, recv_rows, send_sem, recv_sem):
        self.comm, self.send_row, self.recv_rows, self.ss, self.rs = comm, send_row, recv_rows, send_sem, recv_sem

    def copy(self, axis, off):
        n, me = self.comm.counts[axis], self.comm.pos[axis]
        return pltpu.make_async_remote_copy(
            src_ref=self.send_row.at[axis], dst_ref=self.recv_rows[axis].at[me],
            send_sem=self.ss.at[axis, off], recv_sem=self.rs.at[axis, off],
            device_id={AXES[axis]: lax.rem(me + off, n)}, device_id_type=MESH)

    def run(self, row):
        for axis in range(3):
            n, me = self.comm.counts[axis], self.comm.pos[axis]
            rows = self.recv_rows[axis]
            self.send_row[axis] = row
            rows[me] = row
            for off in range(1, n):
                self.copy(axis, off).start()
            for off in range(1, n):
                self.copy(axis, off).wait()
            parts = [rows[i] for i in range(n)]
            row = total_of(parts)
        return row


def store_plane_faces(comm, rnd, ref, p):
    comm.ys[rnd, 0, p] = ref[p + 1, R0:R0 + 1, :]
    comm.ys[rnd, 1, p] = ref[p + 1, R0 + NY - 1:R0 + NY, :]


def pack_x_faces(comm, rnd, ref):
    half = NY // 2
    lane = lane_iota(half)
    a, b = ref[1, R0:R0 + half, :], ref[1, R0 + half:R0 + NY, :]
    comm.xs[rnd, 0] = jnp.where(lane < HALF, a, turn_half(b))
    a, b = ref[NP, R0:R0 + half, :], ref[NP, R0 + half:R0 + NY, :]
    comm.xs[rnd, 1] = jnp.where(lane < HALF, turn_half(a), b)


def z_pack_tile(vals, t, p, acc):
    s = 4 * p + t % 4
    lane = lane_iota() & LOW
    w = pltpu.roll(vals, s, 1)
    e = t // 4
    acc[e] = jnp.where(lane == s, w, acc[e])
    acc[2 + e] = jnp.where(lane == ((s + LOW) & LOW), w, acc[2 + e])


def z_ghost_lo(zr, rnd, t, p):
    s = 4 * p + t % 4
    return pltpu.roll(zr[rnd, 0, t // 4], 65 - s, 1)


def z_ghost_hi(zr, rnd, t, p):
    s = 4 * p + t % 4
    return pltpu.roll(zr[rnd, 1, t // 4], LOW - s, 1)


def unpack_xy(comm, rnd, ref):
    half = NY // 2
    lane = lane_iota(half)
    lo, hi = comm.xr[rnd, 0], comm.xr[rnd, 1]
    top_a, top_b = ref[NP, R0:R0 + half, :], ref[NP, R0 + half:R0 + NY, :]
    ref[0, R0:R0 + half, :] = jnp.where(lane < HALF, lo, turn_half(top_a))
    ref[0, R0 + half:R0 + NY, :] = jnp.where(lane < HALF, turn_half(lo), turn_half(top_b))
    bot_a, bot_b = ref[1, R0:R0 + half, :], ref[1, R0 + half:R0 + NY, :]
    ref[NP + 1, R0:R0 + half, :] = jnp.where(lane < HALF, turn_half(bot_a), turn_half(hi))
    ref[NP + 1, R0 + half:R0 + NY, :] = jnp.where(lane < HALF, turn_half(bot_b), hi)
    for p in range(NP):
        ref[p + 1, R0 - 1:R0, :] = comm.yr[rnd, 0, p]
        ref[p + 1, R0 + NY:R0 + NY + 1, :] = comm.yr[rnd, 1, p]


def neighbours(ref, zr, rnd, p, t):
    row = R0 + 8 * t
    lane = lane_iota() & LOW
    centre = ref[p + 1, row:row + 8, :]
    xm = ref[p, row:row + 8, :]
    xp = ref[p + 2, row:row + 8, :]
    ym = ref[p + 1, row - 1:row + 7, :]
    yp = ref[p + 1, row + 1:row + 9, :]
    zm = jnp.where(lane == 0, z_ghost_lo(zr, rnd, t, p), pltpu.roll(centre, 1, 1))
    zp = jnp.where(lane == LOW, z_ghost_hi(zr, rnd, t, p), pltpu.roll(centre, 127, 1))
    return centre, (xm, xp, ym, yp, zm, zp)


def zero_tiles(n):
    return tuple(jnp.zeros(TILE, F32) for _ in range(n))


def send_faces(comm, rnd, ref, zacc):
    pack_x_faces(comm, rnd, ref)
    for i, part in enumerate(zacc):
        comm.zs[rnd, i // 2, i % 2] = part
    for face in reversed(range(FACES)):
        comm.send(rnd, face)


def load_field(comm, rnd, raw, ref):
    def body(p, zacc):
        zacc = list(zacc)
        ref[p + 1, R0:R0 + NY, :] = jnp.concatenate([raw[p], raw[p + NP]], axis=1)
        for t in range(ROWS):
            z_pack_tile(ref[p + 1, own(t), :], t, p, zacc)
        store_plane_faces(comm, rnd, ref, p)
        return tuple(zacc)
    return lax.fori_loop(0, NP, body, zero_tiles(4))


def fill_ghost_conductivity(comm, gx_slab, gy_slab, gz_slab):
    px, py, pz = comm.pos
    half = NY // 2
    turn = 64 * lax.rem(pz, 2)
    lane = lane_iota(half)
    a, b = pltpu.roll(gx_slab[0:half, :], turn, 1), pltpu.roll(gx_slab[half:NY, :], turn, 1)
    x_face = jnp.where(lane < HALF, a, turn_half(b))
    for end in range(2):
        @pl.when(jnp.logical_not(comm.has[end]))
        def _():
            comm.xr[0, end] = x_face
    rows = pltpu.roll(gy_slab[...], turn, 1)
    y_face = jnp.where(lane_iota(NP) < HALF, rows[0:NP], turn_half(rows[NP:NX]))
    for end in range(2):
        @pl.when(jnp.logical_not(comm.has[2 + end]))
        def _():
            for p in range(NP):
                comm.yr[0, end, p] = y_face[one(p)]
    for end in range(2):
        @pl.when(jnp.logical_not(comm.has[4 + end]))
        def _():
            cols = pltpu.roll(gz_slab[...], 64 * lax.rem(py, 2), 1)
            blank = jnp.zeros((48, LANES), F32)
            square = jnp.concatenate([cols[0:NP], blank, cols[NP:NX], blank], axis=0)
            turned = square.T
            acc = [jnp.zeros(TILE, F32)] * 2
            low = lane_iota() & LOW
            for p in range(NP):
                for t in range(ROWS):
                    s = 4 * p + t % 4
                    at = s if end else s + LOW
                    w = pltpu.roll(turned[tile(t)], (at - p) % 128, 1)
                    acc[t // 4] = jnp.where(low == at % 64, w, acc[t // 4])
            comm.zr[0, end, 0], comm.zr[0, end, 1] = acc[0], acc[1]


def zero_ends(comm, rounds):
    for face in range(FACES):
        @pl.when(jnp.logical_not(comm.has[face]))
        def _():
            buf = (comm.xr, comm.yr, comm.zr)[face // 2]
            for rnd in rounds:
                buf[rnd, face % 2] = jnp.zeros(buf.shape[2:], F32)


def lanes_of(pos):
    return pl.ds(pl.multiple_of(lax.div(pos, 2) * LANES, LANES), LANES)


def start_up(comm, ins, raws, slabs, load_sem):
    k_hbm, g_hbm, f_hbm, u_hbm = ins
    px, py, pz = comm.pos
    loads = [pltpu.make_async_copy(k_hbm, raws[0], load_sem.at[0]),
             pltpu.make_async_copy(u_hbm, raws[1], load_sem.at[1])]
    x_row = jnp.where(comm.has[1], 0, 1)
    y_row = jnp.where(comm.has[3], 2, 3)
    z_row = jnp.where(comm.has[5], 4, 5)
    z_lanes = lanes_of(pz)
    y_lanes = lanes_of(py)
    loads.append(pltpu.make_async_copy(
        g_hbm.at[x_row, pl.ds(pl.multiple_of(py * NY, NY), NY), z_lanes], slabs[0], load_sem.at[2]))
    loads.append(pltpu.make_async_copy(
        g_hbm.at[y_row, pl.ds(pl.multiple_of(px * NX, NX), NX), z_lanes], slabs[1], load_sem.at[3]))
    loads.append(pltpu.make_async_copy(
        g_hbm.at[z_row, pl.ds(pl.multiple_of(px * NX, NX), NX), y_lanes], slabs[2], load_sem.at[4]))
    loads.append(pltpu.make_async_copy(f_hbm, raws[2], load_sem.at[5]))
    for load in loads:
        load.start()
    return loads


def first_exchange(comm, loads, greet, raws, slabs, k_ref, u_ref):
    sem, total = greet
    loads[0].wait()
    zacc = load_field(comm, 0, raws[0], k_ref)
    pl.semaphore_wait(sem, total)
    send_faces(comm, 0, k_ref, zacc)
    loads[1].wait()
    zacc = load_field(comm, 1, raws[1], u_ref)
    send_faces(comm, 1, u_ref, zacc)
    for load in loads[2:]:
        load.wait()
    fill_ghost_conductivity(comm, *slabs)
    for rnd, ref in ((0, k_ref), (1, u_ref)):
        for face in range(FACES):
            comm.wait_recv(rnd, face)
        unpack_xy(comm, rnd, ref)


def first_residual(comm, raw_f, k_ref, u_ref, p, t, scale, coef_ref, d_ref):
    own, others = neighbours(k_ref, comm.zr, 0, p, t)
    u_own, u_others = neighbours(u_ref, comm.zr, 1, p, t)
    twice = own + own
    weights = [twice * other / (own + other) for other in others]
    diag = total_of(weights)
    flux = [w * (u_own - other) for w, other in zip(weights, u_others)]
    au = total_of(flux)
    rows = tile(t)
    inv = 1.0 / diag
    f_tile = jnp.concatenate([raw_f[p, rows, :], raw_f[p + NP, rows, :]], axis=1)
    resid = f_tile - au
    factor = inv + inv if scale else None
    for i in range(FACES):
        coef_ref[i, p, rows, :] = weights[i] * factor if scale else weights[i]
    d_ref[p, rows, :] = diag
    return resid, inv


def write_plane(raw_ref, p, values):
    raw_ref[p] = values[:, :HALF]
    raw_ref[p + NP] = turn_half(values)[:, :HALF]


def dot_rows(a, b):
    prod = a[:2 * SUB] * b[:2 * SUB]
    return row_sum(prod[:SUB] + prod[SUB:])


def solve_coefficients(row, mom_ref, pc_ref, hist_ref, full_ref):
    lane24, line24 = lane_iota(24), row_iota(24)
    wide = jnp.broadcast_to(row, (24, LANES))
    base = lane_sum(jnp.where((lane24 == line24) & (lane24 < 17), wide, 0.0))
    base = jnp.broadcast_to(base, (24, LANES))
    first, second = base[0:1], base[1:2]
    even = (line24 & 1) == 0
    mom = jnp.where(line24 >= 2, 2.0 * base - jnp.where(even, first, second), base)
    mom = jnp.where(line24 < 17, mom, 0.0)
    lane16, line16 = lane_iota(16), row_iota(16)
    wide = jnp.broadcast_to(row, WIDE)
    for k in range(NB):
        big = jnp.maximum(line16, k)
        small = jnp.minimum(line16, k)
        want = 17 + lax.shift_right_logical(big * (big + 1), 1) + small
        col = lane_sum(jnp.where((lane16 == want) & (line16 < NB), wide, 0.0))
        full_ref[k] = jnp.broadcast_to(col, WIDE)
    zeros8 = jnp.zeros(TILE, F32)
    mom_ref[:SUB] = zeros8
    mom_ref[32:40] = zeros8
    pc_ref[:SUB] = zeros8
    pc_ref[24:32] = zeros8
    unit = jnp.where(line16 == 0, 1.0, 0.0)
    cvec, pvec, avec = unit, unit, jnp.zeros(WIDE, F32)
    rvec, mvec = mom, mom
    mu0 = mom[0:1]
    rho = dot_rows(cvec, rvec)
    ok = jnp.where(rho > 0.0, 1.0, 0.0)
    two_one = jnp.where(line16 == 1, 2.0, 1.0)
    for t in range(CG_ITERS):
        mom_ref[8:32] = mvec
        mom_ref[7:8] = mvec[1:2]
        pc_ref[8:24] = pvec
        qvec = mvec - 0.5 * (mom_ref[9:33] + mom_ref[7:31])
        npvec = 0.5 * (two_one * pc_ref[7:23] + pc_ref[9:25])
        curv = dot_rows(pvec, qvec)
        size = row_sum(jnp.abs(pvec))
        ok = jnp.where(size * size * mu0 < BOUND * curv, ok, 0.0)
        alpha = rho / curv
        avec = avec + alpha * pvec
        cvec = cvec - alpha * (pvec - npvec)
        rvec = rvec - alpha * qvec
        hist_ref[t] = cvec
        rho_new = dot_rows(cvec, rvec)
        size = row_sum(jnp.abs(cvec))
        ok = jnp.where(size * size * mu0 < BOUND * rho_new, ok, 0.0)
        beta = rho_new / rho
        pvec = cvec + beta * pvec
        mvec = rvec + beta * mvec
        rho = rho_new
    return avec, cvec, ok


def squares_row(hist_ref, full_ref, ok):
    lane = lane_iota(1)
    out = jnp.where(lane == 8, ok, 0.0)
    for t in range(CG_ITERS):
        cvec = hist_ref[t]
        acc = full_ref[0] * hist_ref[t, one(0)]
        for j in range(1, NB):
            acc = acc + full_ref[j] * hist_ref[t, one(j)]
        out = jnp.where(lane == t, dot_rows(acc, cvec), out)
    return out


def basis_kernel(counts, k_hbm, g_hbm, f_hbm, u_hbm, uo_hbm, ro_hbm, h_ref,
                 raw_k, raw_u, raw_f, slab_x, slab_y, slab_z, k_ref, u_ref, z_ref, coef_ref, d_ref, sums_ref,
                 mom_ref, pc_ref, hist_ref, full_ref, comb_ref,
                 xs, ys, zs, xr, yr, zr, send_row, rows_x, rows_y, rows_z,
                 load_sem, store_sem, send_sem, recv_sem, red_ss, red_rs):
    comm = Comm(counts, (xs, ys, zs, xr, yr, zr, send_sem, recv_sem))
    raws, slabs = (raw_k, raw_u, raw_f), (slab_x, slab_y, slab_z)
    loads = start_up(comm, (k_hbm, g_hbm, f_hbm, u_hbm), raws, slabs, load_sem)
    greet = barrier_all_lines(comm)
    zero_ends(comm, range(1, CG_ITERS + 2))
    sums_ref[...] = jnp.zeros(sums_ref.shape, F32)
    first_exchange(comm, loads, greet, raws, slabs, k_ref, u_ref)

    def first(p, zacc):
        zacc = list(zacc)
        for t in range(ROWS):
            resid, inv = first_residual(comm, raw_f, k_ref, u_ref, p, t, True, coef_ref, d_ref)
            z_new = resid * inv
            z_ref[0, p + 1, own(t), :] = z_new
            z_pack_tile(z_new, t, p, zacc)
        store_plane_faces(comm, 2, z_ref.at[0], p)
        return tuple(zacc)

    zacc = lax.fori_loop(0, NP, first, zero_tiles(4))
    send_faces(comm, 2, z_ref.at[0], zacc)

    def products(k):
        def body(p, accs):
            accs = list(accs)
            for t in range(ROWS):
                row = own(t)
                d = d_ref[p, tile(t), :]
                z_k = z_ref[k, p + 1, row, :]
                dz = d * z_k
                ddz = d * dz
                for i in range(k + 1):
                    z_i = z_ref[i, p + 1, row, :]
                    accs[i] = accs[i] + ddz * z_i
                    if i >= k - 1:
                        accs[k + 1 + (k - i)] = accs[k + 1 + (k - i)] + dz * z_i
            return tuple(accs)
        accs = lax.fori_loop(0, NP, body, zero_tiles(k + 2 + (1 if k else 0)))
        for i in range(k + 1):
            at = 17 + k * (k + 1) // 2 + i
            sums_ref[one(at)] = row_sum(accs[i])
        sums_ref[one(2 * k)] = row_sum(accs[k + 1])
        if k:
            sums_ref[one(2 * k - 1)] = row_sum(accs[k + 2])

    for k in range(CG_ITERS):
        rnd = 2 + k
        products(k)
        for face in range(FACES):
            comm.wait_recv(rnd, face)
        unpack_xy(comm, rnd, z_ref.at[k])
        last = k == CG_ITERS - 1

        def step(p, zacc):
            zacc = list(zacc)
            for t in range(ROWS):
                _, others = neighbours(z_ref.at[k], zr, rnd, p, t)
                rows = tile(t)
                terms = [coef_ref[i, p, rows, :] * others[i] for i in range(FACES)]
                total = total_of(terms)
                row = own(t)
                z_new = 0.5 * total if k == 0 else total - z_ref[k - 1, p + 1, row, :]
                z_ref[k + 1, p + 1, row, :] = z_new
                if not last:
                    z_pack_tile(z_new, t, p, zacc)
            if not last:
                store_plane_faces(comm, rnd + 1, z_ref.at[k + 1], p)
            return tuple(zacc)

        zacc = lax.fori_loop(0, NP, step, zero_tiles(4))
        if not last:
            send_faces(comm, rnd + 1, z_ref.at[k + 1], zacc)
    products(CG_ITERS)

    total = jnp.broadcast_to(lane_sum(sums_ref[...]), (NY, LANES))
    row = row_sum(jnp.where(lane_iota(64) == row_iota(64), total, 0.0))
    red = Reducer(comm, send_row, (rows_x, rows_y, rows_z), red_ss, red_rs)
    row = red.run(row)
    avec, cvec, ok = solve_coefficients(row, mom_ref, pc_ref, hist_ref, full_ref)
    comb_ref[0] = avec
    comb_ref[1] = cvec

    a_co = [jnp.broadcast_to(comb_ref[0, one(i)], TILE) for i in range(CG_ITERS)]
    c_co = [jnp.broadcast_to(comb_ref[1, one(i)], TILE) for i in range(NB)]

    def combine(p, carry):
        for t in range(ROWS):
            row = own(t)
            rows = tile(t)
            basis = [z_ref[i, p + 1, row, :] for i in range(NB)]
            ut, rt = a_co[0] * basis[0], c_co[0] * basis[0]
            for i in range(1, NB):
                if i < CG_ITERS:
                    ut = ut + a_co[i] * basis[i]
                rt = rt + c_co[i] * basis[i]
            ut = u_ref[p + 1, row, :] + ut
            rt = d_ref[p, rows, :] * rt
            raw_u[p, rows, :] = ut[:, :HALF]
            raw_u[p + NP, rows, :] = turn_half(ut)[:, :HALF]
            raw_f[p, rows, :] = rt[:, :HALF]
            raw_f[p + NP, rows, :] = turn_half(rt)[:, :HALF]
        return carry

    lax.fori_loop(0, NP, combine, 0)
    outs = [pltpu.make_async_copy(raw_u, uo_hbm, store_sem.at[0]), pltpu.make_async_copy(raw_f, ro_hbm, store_sem.at[1])]
    for out in outs:
        out.start()
    h_ref[...] = squares_row(hist_ref, full_ref, ok)
    for rnd in range(CG_ITERS + 2):
        for face in range(FACES):
            comm.wait_send(rnd, face)
    for out in outs:
        out.wait()


def plain_kernel(counts, k_hbm, g_hbm, f_hbm, u_hbm, uo_hbm, ro_hbm, h_ref,
                 raw_k, raw_u, raw_f, slab_x, slab_y, slab_z, k_ref, u_ref, p_ref, q_ref, r_ref, coef_ref, d_ref,
                 xs, ys, zs, xr, yr, zr, send_row, rows_x, rows_y, rows_z,
                 load_sem, store_sem, send_sem, recv_sem, red_ss, red_rs):
    comm = Comm(counts, (xs, ys, zs, xr, yr, zr, send_sem, recv_sem))
    raws, slabs = (raw_k, raw_u, raw_f), (slab_x, slab_y, slab_z)
    loads = start_up(comm, (k_hbm, g_hbm, f_hbm, u_hbm), raws, slabs, load_sem)
    greet = barrier_all_lines(comm)
    zero_ends(comm, range(1, 3))
    first_exchange(comm, loads, greet, raws, slabs, k_ref, u_ref)
    red = [Reducer(comm, send_row.at[i], (rows_x.at[i], rows_y.at[i], rows_z.at[i]), red_ss.at[i], red_rs.at[i]) for i in range(2)]

    def reduce(which, accs):
        lane = lane_iota(1)
        row = jnp.zeros((1, LANES), F32)
        for i, acc in enumerate(accs):
            total = row_sum(lane_sum(acc))
            row = jnp.where(lane == i, jnp.broadcast_to(total, (1, LANES)), row)
        row = red[which].run(row)
        return [lane_sum(jnp.where(lane == i, row, 0.0)) for i in range(len(accs))]

    def first(p, accs):
        acc = accs[0]
        for t in range(ROWS):
            resid, inv = first_residual(comm, raw_f, k_ref, u_ref, p, t, False, coef_ref, d_ref)
            rows = tile(t)
            r_ref[p, rows, :] = resid
            z_new = resid * inv
            p_ref[p + 1, own(t), :] = z_new
            acc = acc + resid * z_new
        return (acc,)

    rho, = reduce(0, lax.fori_loop(0, NP, first, zero_tiles(1)))

    def iteration(it, carry):
        rho, hist = carry

        def pack(p, zacc):
            zacc = list(zacc)
            for t in range(ROWS):
                z_pack_tile(p_ref[p + 1, own(t), :], t, p, zacc)
            store_plane_faces(comm, 2, p_ref, p)
            return tuple(zacc)

        send_faces(comm, 2, p_ref, lax.fori_loop(0, NP, pack, zero_tiles(4)))
        for face in range(FACES):
            comm.wait_recv(2, face)
            comm.wait_send(2, face)
        unpack_xy(comm, 2, p_ref)

        def apply(p, accs):
            acc = accs[0]
            for t in range(ROWS):
                own, others = neighbours(p_ref, zr, 2, p, t)
                rows = tile(t)
                flux = [coef_ref[i, p, rows, :] * (own - others[i]) for i in range(FACES)]
                q = total_of(flux)
                q_ref[p, rows, :] = q
                acc = acc + own * q
            return (acc,)

        curv, = reduce(1, lax.fori_loop(0, NP, apply, zero_tiles(1)))
        alpha = jnp.broadcast_to(rho / curv, TILE)

        def update(p, accs):
            acc_z, acc_r = accs
            for t in range(ROWS):
                row = own(t)
                rows = tile(t)
                u_ref[p + 1, row, :] = u_ref[p + 1, row, :] + alpha * p_ref[p + 1, row, :]
                resid = r_ref[p, rows, :] - alpha * q_ref[p, rows, :]
                r_ref[p, rows, :] = resid
                acc_z = acc_z + resid * (resid / d_ref[p, rows, :])
                acc_r = acc_r + resid * resid
            return acc_z, acc_r

        rho_new, rr = reduce(0, lax.fori_loop(0, NP, update, zero_tiles(2)))
        beta = jnp.broadcast_to(rho_new / rho, TILE)

        def turn(p, carry):
            for t in range(ROWS):
                row = own(t)
                rows = tile(t)
                p_ref[p + 1, row, :] = r_ref[p, rows, :] / d_ref[p, rows, :] + beta * p_ref[p + 1, row, :]
            return carry

        lax.fori_loop(0, NP, turn, 0)
        hist = jnp.where(lane_iota(1) == it, jnp.broadcast_to(rr, (1, LANES)), hist)
        return rho_new, hist

    _, hist = lax.fori_loop(0, CG_ITERS, iteration, (rho, jnp.zeros((1, LANES), F32)))
    h_ref[...] = hist

    def finish(p, carry):
        write_plane(raw_u, p, u_ref[p + 1, R0:R0 + NY, :])
        write_plane(raw_f, p, r_ref[p])
        return carry

    lax.fori_loop(0, NP, finish, 0)
    outs = [pltpu.make_async_copy(raw_u, uo_hbm, store_sem.at[0]), pltpu.make_async_copy(raw_f, ro_hbm, store_sem.at[1])]
    for out in outs:
        out.start()
    for rnd in range(2):
        for face in range(FACES):
            comm.wait_send(rnd, face)
    for out in outs:
        out.wait()


def scratch_for(kind, counts):
    field = (NP + 2, NY + 16, LANES)
    block = (NP, NY, LANES)
    vm = lambda *shape: pltpu.VMEM(shape, F32)
    raws = [vm(NX, NY, NZ)] * 3 + [vm(NY, LANES), vm(NX, LANES), vm(NX, LANES)]
    if kind == 'basis':
        rounds, reds = CG_ITERS + 2, ()
        work = [vm(*field), vm(*field), vm(NB, *field), vm(6, *block), vm(*block), vm(NY, LANES),
                vm(40, LANES), vm(32, LANES), vm(CG_ITERS, 16, LANES), vm(NB, 16, LANES), vm(2, 16, LANES)]
    else:
        rounds, reds = 3, (2,)
        work = [vm(*field), vm(*field), vm(*field), vm(*block), vm(*block), vm(6, *block), vm(*block)]
    faces = [vm(rounds, 2, NY // 2, LANES), vm(rounds, 2, NP, 1, LANES), vm(rounds, 2, 2, 8, LANES)] * 2
    rows = [vm(*reds, 3, 1, LANES)] + [vm(*reds, n, 1, LANES) for n in counts]
    dma = pltpu.SemaphoreType.DMA
    sems = [dma((6,)), dma((2,)), dma((rounds, 6)), dma((rounds, 6)), dma((*reds, 3, 8)), dma((*reds, 3, 8))]
    return raws + work + faces + rows + sems


def solution(mesh):
    counts = tuple(mesh.shape[name] for name in AXES)
    grid_spec = P(*AXES)
    block = jax.ShapeDtypeStruct((NX, NY, NZ), F32)

    def call(kernel, kind, ident):
        hbm = pl.BlockSpec(memory_space=pl.ANY)
        return pl.pallas_call(
            functools.partial(kernel, counts),
            out_shape=(block, block, jax.ShapeDtypeStruct((1, LANES), F32)),
            in_specs=[hbm] * 4,
            out_specs=(hbm, hbm, pl.BlockSpec(memory_space=pltpu.VMEM)),
            scratch_shapes=scratch_for(kind, counts),
            compiler_params=pltpu.CompilerParams(collective_id=ident, has_side_effects=True),
            name=kind,
        )

    def local_solve(k_cell, k_ghost, f_rhs, u_init):
        args = (k_cell, k_ghost, f_rhs, u_init)
        u_out, r_out, row = call(basis_kernel, 'basis', 0)(*args)
        u_out, r_out, row = lax.cond(
            row[0, 8] > 0.5,
            lambda: (u_out, r_out, row),
            lambda: tuple(call(plain_kernel, 'plain', 1)(*args)))
        return u_out, r_out, row[0, 0:CG_ITERS]

    return jax.shard_map(local_solve, mesh=mesh, in_specs=(grid_spec, P(), grid_spec, grid_spec),
                         out_specs=(grid_spec, grid_spec, P()), check_vma=False)
```

time: 1460 us -> 324 us (0.22)
  blocking collectives: 1020 us -> 0 us
  Pallas kernels: 0 us -> 318 us
  starting transfers between devices: 162 us -> 0 us
  other arithmetic: 119 us -> 0 us
  local copies, waits for them, and re-layouts: 120 us -> 4.63 us
  between operations: 21.8 us -> 1.33 us
    psum x16 -> x0, blocking collectives: 1020 us -> none  [global_sum(): return lax.psum(local_value, MESH_AXES)]
    pallas_call x0 -> x2, Pallas kernels: none -> 318 us  [the longest x1 240 us: local_solve(): call(plain_kernel, 'plain', 1)(*args)]
    ppermute x60 -> x0, starting transfers between devices: 162 us -> none  [the longest x30 124 us: neighbour_layers(): from_below = lax.ppermute(top_layer, GRID_AXES[axis_dim], upward)]
    slice x55 -> x1, local copies, waits for them, and re-layouts: 62.7 us -> 0.58 us  [local_solve(): row[0, 8] > 0.5]
    reduce_sum x16 -> x0, other arithmetic: 47.7 us -> none  [the longest x8 30.5 us: local_solve(): jnp.sum(residual * precond)]
    mul x28 -> x0, other arithmetic: 44.2 us -> none  [the longest x27 41.5 us: apply_operator(): face_coefs[axis_dim]]
    ppermute x18 -> x0, local copies, waits for them, and re-layouts: 34.1 us -> none  [the longest x9 17.1 us: neighbour_layers(): from_below = lax.ppermute(top_layer, GRID_AXES[axis_dim], upward)]
    add x8 -> x0, other arithmetic: 15.8 us -> none  [the longest x7 11.7 us: local_solve(): direction = precond + pair_sums[0] / rz_old * direction]
  transfers between devices with their start and end apart: 60 -> 0, of which waited for: 2 -> 0; matrix products, arithmetic and copies ran while one was open for 7% -> 0% of each run, Pallas kernels for 0% -> 0%
where the time goes in v1:
time: 324 us
  Pallas kernels  318 us (98%)
  local copies, waits for them, and re-layouts  4.63 us (1%)
    pallas_call x1, Pallas kernels, local_solve(): call(plain_kernel, 'plain', 1)(*args)  240 us
    pallas_call x1, Pallas kernels, local_solve(): u_out, r_out, row = call(basis_kernel, 'basis', 0)(*args)  77.8 us

profile of v1, /device:TPU:0, one launch (start us, length us, event | category | flops | bytes accessed | tf_op | source)
XLA Modules:
  0.0 323.5 jit_solution(10566422092075259599)
XLA Ops:
  0.6 0.0 copy-start
  0.6 0.0 copy-start.1
  0.6 77.8 %basis.1 = (f32[32,64,64]{2,1,0:T(8,128)}, f32[32,64,64]{2,1,0:T(8,128)}, f32[1,128]{1,0:T(1,128)S(1)}) custom-call(f32[32,64,64]{2,1,0:T(8,128)} %k_hbm.1, f32[6,256,256]{2,1,0:T(8,128)} %g_hbm.1, f32[32,64,64]{2,1,0:T(8,128)} %f_hbm.1, f32[32,64,64]{2,1,0:T(8,128)} %u_hbm.1), custom_call_target="tpu_custom_call" | custom-call | tf_op jit(solution)/shard_map/basis/pallas_call | solution.py:683
  78.5 0.6 slice.10
  79.7 0.0 copy-done
  79.7 0.0 copy-done.1
  79.7 240.4 %conditional.1 = (f32[32,64,64]{2,1,0:T(8,128)}, f32[32,64,64]{2,1,0:T(8,128)}, f32[8]{0:T(128)S(1)}) conditional(s32[]{:T(128)} %bitcast.2, (f32[32,64,64]{2,1,0:T(8,128)S(1)}, f32[6,256,256]{2,1,0:T(8,128)S(1)}, f32[32,64,64]{2,1,0:T(8,128)}, f32[32,64,64]{2,1,0:T(8,128)}) %tuple.29, (f32[1,128]{1,0:T(1,128)S(1)}, f32[32,64,64]{2,1,0:T(8,128)}, ...), branch_computations={%region_0.0_spmd, %region_1.0_spmd} | conditional | bytes 88 | solution.py:684
  79.8 239.7 %plain.1 = (f32[32,64,64]{2,1,0:T(8,128)}, f32[32,64,64]{2,1,0:T(8,128)}, f32[1,128]{1,0:T(1,128)}) custom-call(f32[32,64,64]{2,1,0:T(8,128)S(1)} %get-tuple-element.21.k_hbm, f32[6,256,256]{2,1,0:T(8,128)S(1)} %get-tuple-element.22.g_hbm, f32[32,64,64]{2,1,0:T(8,128)} %get-tuple-element.23.f_hbm, f32[32,64,64]{2,1,0:T(8,128)} %get-tuple-element.24.u_hbm), custom_call_target="tpu_custom_call" | custom-call | tf_op jit(solution)/shard_map/cond/branch_0_fun/plain/pallas_call | solution.py:687
  319.5 0.7 slice_bitcast_fusion
  320.2 0.0 copy-start.3
  320.2 0.0 copy-start.2
  320.2 2.4 copy.15
  322.6 0.0 copy-done.2
  322.6 1.0 copy.16
  323.5 0.0 copy-done.3
Async XLA Ops:
  0.6 79.1 %copy-start = (f32[6,256,256]{2,1,0:T(8,128)S(1)}, f32[6,256,256]{2,1,0:T(8,128)}, u32[]{:S(2)}) copy-start(f32[6,256,256]{2,1,0:T(8,128)} %g_hbm.1) | copy-start | bytes 4718596
  0.6 79.1 %copy-start.1 = (f32[32,64,64]{2,1,0:T(8,128)S(1)}, f32[32,64,64]{2,1,0:T(8,128)}, u32[]{:S(2)}) copy-start(f32[32,64,64]{2,1,0:T(8,128)} %k_hbm.1) | copy-start | bytes 1572868
  320.2 3.4 %copy-start.3 = (f32[8]{0:T(128)}, f32[8]{0:T(128)S(1)}, u32[]{:S(2)}) copy-start(f32[8]{0:T(128)S(1)} %get-tuple-element.58) | copy-start | bytes 100
  320.2 2.4 copy-start.2

commit v2 on v1

--- a/solution.py
+++ b/solution.py
@@ -21,6 +21,8 @@
 TILE = (SUB, LANES)
 WIDE = (2 * SUB, LANES)
 FACES = 6
+FOLD = NY // 2
+TURNS = (4, 8, 16, 32)
 
 
 def own(t):
@@ -76,13 +78,17 @@
             self.has.append(self.pos[axis] < counts[axis] - 1)
         (self.xs, self.ys, self.zs, self.xr, self.yr, self.zr, self.send_sem, self.recv_sem) = bufs
 
+    def source(self, rnd, face):
+        axis, high = face // 2, face % 2
+        return self.zs.at[rnd] if axis == 2 else (self.xs, self.ys)[axis].at[rnd, high]
+
     def copies(self, rnd, face):
         axis, high = face // 2, face % 2
-        src = (self.xs, self.ys, self.zs)[axis]
+        src = self.source(rnd, face)
         dst = (self.xr, self.yr, self.zr)[axis]
         step = 1 if high else -1
         return pltpu.make_async_remote_copy(
-            src_ref=src.at[rnd, high], dst_ref=dst.at[rnd, 1 - high],
+            src_ref=src, dst_ref=dst.at[rnd, 1 - high],
             send_sem=self.send_sem.at[rnd, face], recv_sem=self.recv_sem.at[rnd, face ^ 1],
             device_id={AXES[axis]: self.pos[axis] + step}, device_id_type=MESH)
 
@@ -93,14 +99,14 @@
 
     def wait_recv(self, rnd, face):
         axis, high = face // 2, face % 2
-        src = (self.xs, self.ys, self.zs)[axis]
+        src = self.source(rnd, face)
         dst = (self.xr, self.yr, self.zr)[axis]
         step = 1 if high else -1
 
         @pl.when(self.has[face])
         def _():
             pltpu.make_async_remote_copy(
-                src_ref=src.at[rnd, high], dst_ref=dst.at[rnd, high],
+                src_ref=src, dst_ref=dst.at[rnd, high],
                 send_sem=self.send_sem.at[rnd, face], recv_sem=self.recv_sem.at[rnd, face],
                 device_id={AXES[axis]: self.pos[axis] + step}, device_id_type=MESH).wait_recv()
 
@@ -153,7 +159,7 @@
 
 
 def pack_x_faces(comm, rnd, ref):
-    half = NY // 2
+    half = FOLD
     lane = lane_iota(half)
     a, b = ref[1, R0:R0 + half, :], ref[1, R0 + half:R0 + NY, :]
     comm.xs[rnd, 0] = jnp.where(lane < HALF, a, turn_half(b))
@@ -161,79 +167,120 @@
     comm.xs[rnd, 1] = jnp.where(lane < HALF, turn_half(a), b)
 
 
-def z_pack_tile(vals, t, p, acc):
-    s = 4 * p + t % 4
-    lane = lane_iota() & LOW
-    w = pltpu.roll(vals, s, 1)
-    e = t // 4
-    acc[e] = jnp.where(lane == s, w, acc[e])
-    acc[2 + e] = jnp.where(lane == ((s + LOW) & LOW), w, acc[2 + e])
-
-
-def z_ghost_lo(zr, rnd, t, p):
-    s = 4 * p + t % 4
-    return pltpu.roll(zr[rnd, 0, t // 4], 65 - s, 1)
-
-
-def z_ghost_hi(zr, rnd, t, p):
-    s = 4 * p + t % 4
-    return pltpu.roll(zr[rnd, 1, t // 4], LOW - s, 1)
-
-
-def unpack_xy(comm, rnd, ref):
-    half = NY // 2
-    lane = lane_iota(half)
+def face_mask(turn):
+    return ((lane_iota(FOLD) + 1) & LOW) < turn
+
+
+def pack_z(comm, rnd, ref, tree):
+    def fold(p, carry):
+        low, high = ref[p + 1, R0:R0 + FOLD, :], ref[p + 1, R0 + FOLD:R0 + NY, :]
+        tree[p] = jnp.where(face_mask(2), low, spin(high, 2))
+        return carry
+    lax.fori_loop(0, NP, fold, 0, unroll=8)
+    parts = [tree[p] for p in range(NP)]
+    for turn in TURNS:
+        parts = [jnp.where(face_mask(turn), parts[i], spin(parts[i + 1], turn)) for i in range(0, len(parts), 2)]
+    comm.zs[rnd] = parts[0]
+
+
+def unpack_z(comm, rnd, tree):
+    odd = (lane_iota(FOLD) & 1) == 1
+    parts = [jnp.where(odd, spin(comm.zr[rnd, 1], LOW), spin(comm.zr[rnd, 0], HALF + 1))]
+    for turn in reversed(TURNS):
+        parts = [q for part in parts for q in (part, spin(part, LANES - turn))]
+    for p in range(NP):
+        tree[p] = parts[p]
+
+
+def spread_z(comm, rnd, tree, ghost):
+    unpack_z(comm, rnd, tree)
+
+    def fold(p, carry):
+        ghost[p, 0:FOLD, :] = tree[p]
+        ghost[p, FOLD:NY, :] = spin(tree[p], LANES - 2)
+        return carry
+    lax.fori_loop(0, NP, fold, 0, unroll=8)
+
+
+def inner_planes(ref):
+    low = lane_iota(NY) < HALF
+    ref[0, R0:R0 + NY, :] = jnp.where(low, 0.0, turn_half(ref[NP, R0:R0 + NY, :]))
+    ref[NP + 1, R0:R0 + NY, :] = jnp.where(low, turn_half(ref[1, R0:R0 + NY, :]), 0.0)
+
+
+def x_ghosts(comm, rnd):
+    low = lane_iota(FOLD) < HALF
     lo, hi = comm.xr[rnd, 0], comm.xr[rnd, 1]
-    top_a, top_b = ref[NP, R0:R0 + half, :], ref[NP, R0 + half:R0 + NY, :]
-    ref[0, R0:R0 + half, :] = jnp.where(lane < HALF, lo, turn_half(top_a))
-    ref[0, R0 + half:R0 + NY, :] = jnp.where(lane < HALF, turn_half(lo), turn_half(top_b))
-    bot_a, bot_b = ref[1, R0:R0 + half, :], ref[1, R0 + half:R0 + NY, :]
-    ref[NP + 1, R0:R0 + half, :] = jnp.where(lane < HALF, turn_half(bot_a), turn_half(hi))
-    ref[NP + 1, R0 + half:R0 + NY, :] = jnp.where(lane < HALF, turn_half(bot_b), hi)
+    below = [jnp.where(low, lo, 0.0), jnp.where(low, turn_half(lo), 0.0)]
+    above = [jnp.where(low, 0.0, turn_half(hi)), jnp.where(low, 0.0, hi)]
+    return below, above
+
+
+def outer_layers(comm, rnd, ref):
+    inner_planes(ref)
+    below, above = x_ghosts(comm, rnd)
+    for i in range(2):
+        rows = slice(R0 + FOLD * i, R0 + FOLD * i + FOLD)
+        ref[0, rows, :] = ref[0, rows, :] + below[i]
+        ref[NP + 1, rows, :] = ref[NP + 1, rows, :] + above[i]
     for p in range(NP):
         ref[p + 1, R0 - 1:R0, :] = comm.yr[rnd, 0, p]
         ref[p + 1, R0 + NY:R0 + NY + 1, :] = comm.yr[rnd, 1, p]
 
 
-def neighbours(ref, zr, rnd, p, t):
-    row = R0 + 8 * t
+def blank_rows(ref):
+    for p in range(NP):
+        ref[p + 1, R0 - 1:R0, :] = jnp.zeros((1, LANES), F32)
+        ref[p + 1, R0 + NY:R0 + NY + 1, :] = jnp.zeros((1, LANES), F32)
+
+
+def neighbours(ref, p, t, ghost=None):
+    row = R0 + SUB * t
     lane = lane_iota() & LOW
-    centre = ref[p + 1, row:row + 8, :]
-    xm = ref[p, row:row + 8, :]
-    xp = ref[p + 2, row:row + 8, :]
-    ym = ref[p + 1, row - 1:row + 7, :]
-    yp = ref[p + 1, row + 1:row + 9, :]
-    zm = jnp.where(lane == 0, z_ghost_lo(zr, rnd, t, p), pltpu.roll(centre, 1, 1))
-    zp = jnp.where(lane == LOW, z_ghost_hi(zr, rnd, t, p), pltpu.roll(centre, 127, 1))
+    centre = ref[p + 1, own(t), :]
+    xm = ref[p, own(t), :]
+    xp = ref[p + 2, own(t), :]
+    ym = ref[p + 1, row - 1:row + SUB - 1, :]
+    yp = ref[p + 1, row + 1:row + SUB + 1, :]
+    zm, zp = spin(centre, 1), spin(centre, LANES - 1)
+    if ghost is not None:
+        edge = ghost[p, tile(t), :]
+        zm, zp = jnp.where(lane == 0, edge, zm), jnp.where(lane == LOW, edge, zp)
     return centre, (xm, xp, ym, yp, zm, zp)
+
+
+def sweep(body, state=(), unroll=2):
+    def plane(p, carry):
+        carry = list(carry)
+        body(p, carry)
+        return tuple(carry)
+    return lax.fori_loop(0, NP, plane, tuple(state), unroll=unroll)
 
 
 def zero_tiles(n):
     return tuple(jnp.zeros(TILE, F32) for _ in range(n))
 
 
-def send_faces(comm, rnd, ref, zacc):
+def send_faces(comm, rnd, ref, tree):
+    pack_z(comm, rnd, ref, tree)
+    for face in (4, 5):
+        comm.send(rnd, face)
     pack_x_faces(comm, rnd, ref)
-    for i, part in enumerate(zacc):
-        comm.zs[rnd, i // 2, i % 2] = part
-    for face in reversed(range(FACES)):
+    for p in range(NP):
+        store_plane_faces(comm, rnd, ref, p)
+    for face in range(4):
         comm.send(rnd, face)
 
 
-def load_field(comm, rnd, raw, ref):
-    def body(p, zacc):
-        zacc = list(zacc)
+def load_field(raw, ref):
+    def body(p, state):
         ref[p + 1, R0:R0 + NY, :] = jnp.concatenate([raw[p], raw[p + NP]], axis=1)
-        for t in range(ROWS):
-            z_pack_tile(ref[p + 1, own(t), :], t, p, zacc)
-        store_plane_faces(comm, rnd, ref, p)
-        return tuple(zacc)
-    return lax.fori_loop(0, NP, body, zero_tiles(4))
-
-
-def fill_ghost_conductivity(comm, gx_slab, gy_slab, gz_slab):
+    sweep(body, unroll=4)
+
+
+def fill_ghost_conductivity(comm, square, gx_slab, gy_slab, gz_slab):
     px, py, pz = comm.pos
-    half = NY // 2
+    half = FOLD
     turn = 64 * lax.rem(pz, 2)
     lane = lane_iota(half)
     a, b = pltpu.roll(gx_slab[0:half, :], turn, 1), pltpu.roll(gx_slab[half:NY, :], turn, 1)
@@ -252,19 +299,15 @@
     for end in range(2):
         @pl.when(jnp.logical_not(comm.has[4 + end]))
         def _():
-            cols = pltpu.roll(gz_slab[...], 64 * lax.rem(py, 2), 1)
-            blank = jnp.zeros((48, LANES), F32)
-            square = jnp.concatenate([cols[0:NP], blank, cols[NP:NX], blank], axis=0)
-            turned = square.T
-            acc = [jnp.zeros(TILE, F32)] * 2
-            low = lane_iota() & LOW
-            for p in range(NP):
-                for t in range(ROWS):
-                    s = 4 * p + t % 4
-                    at = s if end else s + LOW
-                    w = pltpu.roll(turned[tile(t)], (at - p) % 128, 1)
-                    acc[t // 4] = jnp.where(low == at % 64, w, acc[t // 4])
-            comm.zr[0, end, 0], comm.zr[0, end, 1] = acc[0], acc[1]
+            cols = spin(gz_slab[...], HALF * lax.rem(py, 2))
+            shift = 0 if end else LOW
+            square[...] = jnp.zeros(square.shape, F32)
+            for x in range(NX):
+                for c in range(2):
+                    square[one((4 * (x % NP) + 2 * c + HALF * (x // NP) + shift) % LANES)] = cols[one(x)]
+            turned = square[...].T
+            second = ((lane_iota(FOLD) - shift) & 3) == 2
+            comm.zr[0, end] = jnp.where(second, turned[FOLD:NY], turned[:FOLD])
 
 
 def zero_ends(comm, rounds):
@@ -302,41 +345,35 @@
     return loads
 
 
-def first_exchange(comm, loads, greet, raws, slabs, k_ref, u_ref):
+def first_exchange(comm, loads, greet, raws, slabs, k_ref, u_ref, tree, square, k_ghost, u_ghost):
     sem, total = greet
     loads[0].wait()
-    zacc = load_field(comm, 0, raws[0], k_ref)
+    load_field(raws[0], k_ref)
     pl.semaphore_wait(sem, total)
-    send_faces(comm, 0, k_ref, zacc)
+    send_faces(comm, 0, k_ref, tree)
     loads[1].wait()
-    zacc = load_field(comm, 1, raws[1], u_ref)
-    send_faces(comm, 1, u_ref, zacc)
+    load_field(raws[1], u_ref)
+    send_faces(comm, 1, u_ref, tree)
     for load in loads[2:]:
         load.wait()
-    fill_ghost_conductivity(comm, *slabs)
-    for rnd, ref in ((0, k_ref), (1, u_ref)):
+    fill_ghost_conductivity(comm, square, *slabs)
+    for rnd, ref, ghost in ((0, k_ref, k_ghost), (1, u_ref, u_ghost)):
         for face in range(FACES):
             comm.wait_recv(rnd, face)
-        unpack_xy(comm, rnd, ref)
-
-
-def first_residual(comm, raw_f, k_ref, u_ref, p, t, scale, coef_ref, d_ref):
-    own, others = neighbours(k_ref, comm.zr, 0, p, t)
-    u_own, u_others = neighbours(u_ref, comm.zr, 1, p, t)
-    twice = own + own
-    weights = [twice * other / (own + other) for other in others]
+        outer_layers(comm, rnd, ref)
+        spread_z(comm, rnd, tree, ghost)
+
+
+def first_residual(raw_f, k_ref, u_ref, k_ghost, u_ghost, p, t, d_ref):
+    centre, others = neighbours(k_ref, p, t, k_ghost)
+    u_own, u_others = neighbours(u_ref, p, t, u_ghost)
+    twice = centre + centre
+    weights = [twice * other / (centre + other) for other in others]
     diag = total_of(weights)
-    flux = [w * (u_own - other) for w, other in zip(weights, u_others)]
-    au = total_of(flux)
-    rows = tile(t)
-    inv = 1.0 / diag
-    f_tile = jnp.concatenate([raw_f[p, rows, :], raw_f[p + NP, rows, :]], axis=1)
-    resid = f_tile - au
-    factor = inv + inv if scale else None
-    for i in range(FACES):
-        coef_ref[i, p, rows, :] = weights[i] * factor if scale else weights[i]
-    d_ref[p, rows, :] = diag
-    return resid, inv
+    au = total_of([w * (u_own - other) for w, other in zip(weights, u_others)])
+    f_tile = jnp.concatenate([raw_f[p, tile(t), :], raw_f[p + NP, tile(t), :]], axis=1)
+    d_ref[p, tile(t), :] = diag
+    return weights, f_tile - au, 1.0 / diag
 
 
 def write_plane(raw_ref, p, values):
@@ -416,7 +453,7 @@
 
 def basis_kernel(counts, k_hbm, g_hbm, f_hbm, u_hbm, uo_hbm, ro_hbm, h_ref,
                  raw_k, raw_u, raw_f, slab_x, slab_y, slab_z, k_ref, u_ref, z_ref, coef_ref, d_ref, sums_ref,
-                 mom_ref, pc_ref, hist_ref, full_ref, comb_ref,
+                 mom_ref, pc_ref, hist_ref, full_ref, comb_ref, edge_ref, tree, square, k_ghost, u_ghost,
                  xs, ys, zs, xr, yr, zr, send_row, rows_x, rows_y, rows_z,
                  load_sem, store_sem, send_sem, recv_sem, red_ss, red_rs):
     comm = Comm(counts, (xs, ys, zs, xr, yr, zr, send_sem, recv_sem))
@@ -425,20 +462,25 @@
     greet = barrier_all_lines(comm)
     zero_ends(comm, range(1, CG_ITERS + 2))
     sums_ref[...] = jnp.zeros(sums_ref.shape, F32)
-    first_exchange(comm, loads, greet, raws, slabs, k_ref, u_ref)
-
-    def first(p, zacc):
-        zacc = list(zacc)
+    for k in range(CG_ITERS):
+        blank_rows(z_ref.at[k])
+    first_exchange(comm, loads, greet, raws, slabs, k_ref, u_ref, tree, square, k_ghost, u_ghost)
+
+    def first(p, state):
+        lane = lane_iota() & LOW
         for t in range(ROWS):
-            resid, inv = first_residual(comm, raw_f, k_ref, u_ref, p, t, True, coef_ref, d_ref)
-            z_new = resid * inv
-            z_ref[0, p + 1, own(t), :] = z_new
-            z_pack_tile(z_new, t, p, zacc)
-        store_plane_faces(comm, 2, z_ref.at[0], p)
-        return tuple(zacc)
-
-    zacc = lax.fori_loop(0, NP, first, zero_tiles(4))
-    send_faces(comm, 2, z_ref.at[0], zacc)
+            weights, resid, inv = first_residual(raw_f, k_ref, u_ref, k_ghost, u_ghost, p, t, d_ref)
+            factor = inv + inv
+            scaled = [w * factor for w in weights]
+            low, high = scaled[4:]
+            edge_ref[p, tile(t), :] = jnp.where(lane == 0, low, jnp.where(lane == LOW, high, 0.0))
+            scaled[4:] = jnp.where(lane == 0, 0.0, low), jnp.where(lane == LOW, 0.0, high)
+            for i in range(FACES):
+                coef_ref[p, t, i] = scaled[i]
+            z_ref[0, p + 1, own(t), :] = resid * inv
+
+    sweep(first)
+    send_faces(comm, 2, z_ref.at[0], tree)
 
     def products(k):
         def body(p, accs):
@@ -463,33 +505,47 @@
         if k:
             sums_ref[one(2 * k - 1)] = row_sum(accs[k + 2])
 
+    def late_terms(k, rnd):
+        ref = z_ref.at[k + 1]
+        weigh = (lambda term: 0.5 * term) if k == 0 else (lambda term: term)
+        unpack_z(comm, rnd, tree)
+        below, above = x_ghosts(comm, rnd)
+        for t in range(ROWS):
+            part = slice(SUB * (t % 4), SUB * (t % 4) + SUB)
+            for plane, face, layer in ((1, 0, below), (NP, 1, above)):
+                term = coef_ref[plane - 1, t, face] * layer[t // 4][part]
+                ref[plane, own(t), :] = ref[plane, own(t), :] + weigh(term)
+
+        def body(p, state):
+            for end, t, sub in ((0, 0, 0), (1, ROWS - 1, SUB - 1)):
+                row = R0 + SUB * t + sub
+                term = coef_ref[p, t, 2 + end, one(sub), :] * comm.yr[rnd, end, p]
+                ref[p + 1, one(row), :] = ref[p + 1, one(row), :] + weigh(term)
+            for i in range(2):
+                rows = slice(R0 + FOLD * i, R0 + FOLD * i + FOLD)
+                ghost = spin(tree[p], LANES - 2) if i else tree[p]
+                term = edge_ref[p, FOLD * i:FOLD * i + FOLD, :] * ghost
+                ref[p + 1, rows, :] = ref[p + 1, rows, :] + weigh(term)
+        sweep(body, unroll=4)
+
     for k in range(CG_ITERS):
         rnd = 2 + k
+        inner_planes(z_ref.at[k])
+
+        def step(p, state):
+            for t in range(ROWS):
+                _, others = neighbours(z_ref.at[k], p, t)
+                total = total_of(coef_ref[p, t, i] * others[i] for i in range(FACES))
+                z_new = 0.5 * total if k == 0 else total - z_ref[k - 1, p + 1, own(t), :]
+                z_ref[k + 1, p + 1, own(t), :] = z_new
+
+        sweep(step)
         products(k)
         for face in range(FACES):
             comm.wait_recv(rnd, face)
-        unpack_xy(comm, rnd, z_ref.at[k])
-        last = k == CG_ITERS - 1
-
-        def step(p, zacc):
-            zacc = list(zacc)
-            for t in range(ROWS):
-                _, others = neighbours(z_ref.at[k], zr, rnd, p, t)
-                rows = tile(t)
-                terms = [coef_ref[i, p, rows, :] * others[i] for i in range(FACES)]
-                total = total_of(terms)
-                row = own(t)
-                z_new = 0.5 * total if k == 0 else total - z_ref[k - 1, p + 1, row, :]
-                z_ref[k + 1, p + 1, row, :] = z_new
-                if not last:
-                    z_pack_tile(z_new, t, p, zacc)
-            if not last:
-                store_plane_faces(comm, rnd + 1, z_ref.at[k + 1], p)
-            return tuple(zacc)
-
-        zacc = lax.fori_loop(0, NP, step, zero_tiles(4))
-        if not last:
-            send_faces(comm, rnd + 1, z_ref.at[k + 1], zacc)
+        late_terms(k, rnd)
+        if k < CG_ITERS - 1:
+            send_faces(comm, rnd + 1, z_ref.at[k + 1], tree)
     products(CG_ITERS)
 
     total = jnp.broadcast_to(lane_sum(sums_ref[...]), (NY, LANES))
@@ -534,7 +590,7 @@
 
 
 def plain_kernel(counts, k_hbm, g_hbm, f_hbm, u_hbm, uo_hbm, ro_hbm, h_ref,
-                 raw_k, raw_u, raw_f, slab_x, slab_y, slab_z, k_ref, u_ref, p_ref, q_ref, r_ref, coef_ref, d_ref,
+                 raw_k, raw_u, raw_f, slab_x, slab_y, slab_z, k_ref, u_ref, p_ref, q_ref, r_ref, coef_ref, d_ref, tree, square, k_ghost, u_ghost,
                  xs, ys, zs, xr, yr, zr, send_row, rows_x, rows_y, rows_z,
                  load_sem, store_sem, send_sem, recv_sem, red_ss, red_rs):
     comm = Comm(counts, (xs, ys, zs, xr, yr, zr, send_sem, recv_sem))
@@ -542,7 +598,7 @@
     loads = start_up(comm, (k_hbm, g_hbm, f_hbm, u_hbm), raws, slabs, load_sem)
     greet = barrier_all_lines(comm)
     zero_ends(comm, range(1, 3))
-    first_exchange(comm, loads, greet, raws, slabs, k_ref, u_ref)
+    first_exchange(comm, loads, greet, raws, slabs, k_ref, u_ref, tree, square, k_ghost, u_ghost)
     red = [Reducer(comm, send_row.at[i], (rows_x.at[i], rows_y.at[i], rows_z.at[i]), red_ss.at[i], red_rs.at[i]) for i in range(2)]
 
     def reduce(which, accs):
@@ -554,47 +610,36 @@
         row = red[which].run(row)
         return [lane_sum(jnp.where(lane == i, row, 0.0)) for i in range(len(accs))]
 
-    def first(p, accs):
-        acc = accs[0]
+    def first(p, state):
         for t in range(ROWS):
-            resid, inv = first_residual(comm, raw_f, k_ref, u_ref, p, t, False, coef_ref, d_ref)
-            rows = tile(t)
-            r_ref[p, rows, :] = resid
+            weights, resid, inv = first_residual(raw_f, k_ref, u_ref, k_ghost, u_ghost, p, t, d_ref)
+            for i in range(FACES):
+                coef_ref[p, t, i] = weights[i]
+            r_ref[p, tile(t), :] = resid
             z_new = resid * inv
             p_ref[p + 1, own(t), :] = z_new
-            acc = acc + resid * z_new
-        return (acc,)
-
-    rho, = reduce(0, lax.fori_loop(0, NP, first, zero_tiles(1)))
+            state[0] = state[0] + resid * z_new
+
+    rho, = reduce(0, sweep(first, zero_tiles(1)))
 
     def iteration(it, carry):
         rho, hist = carry
 
-        def pack(p, zacc):
-            zacc = list(zacc)
-            for t in range(ROWS):
-                z_pack_tile(p_ref[p + 1, own(t), :], t, p, zacc)
-            store_plane_faces(comm, 2, p_ref, p)
-            return tuple(zacc)
-
-        send_faces(comm, 2, p_ref, lax.fori_loop(0, NP, pack, zero_tiles(4)))
+        send_faces(comm, 2, p_ref, tree)
         for face in range(FACES):
             comm.wait_recv(2, face)
             comm.wait_send(2, face)
-        unpack_xy(comm, 2, p_ref)
-
-        def apply(p, accs):
-            acc = accs[0]
+        outer_layers(comm, 2, p_ref)
+        spread_z(comm, 2, tree, k_ghost)
+
+        def apply(p, state):
             for t in range(ROWS):
-                own, others = neighbours(p_ref, zr, 2, p, t)
-                rows = tile(t)
-                flux = [coef_ref[i, p, rows, :] * (own - others[i]) for i in range(FACES)]
-                q = total_of(flux)
-                q_ref[p, rows, :] = q
-                acc = acc + own * q
-            return (acc,)
-
-        curv, = reduce(1, lax.fori_loop(0, NP, apply, zero_tiles(1)))
+                centre, others = neighbours(p_ref, p, t, k_ghost)
+                q = total_of(coef_ref[p, t, i] * (centre - others[i]) for i in range(FACES))
+                q_ref[p, tile(t), :] = q
+                state[0] = state[0] + centre * q
+
+        curv, = reduce(1, sweep(apply, zero_tiles(1)))
         alpha = jnp.broadcast_to(rho / curv, TILE)
 
         def update(p, accs):
@@ -649,12 +694,14 @@
     raws = [vm(NX, NY, NZ)] * 3 + [vm(NY, LANES), vm(NX, LANES), vm(NX, LANES)]
     if kind == 'basis':
         rounds, reds = CG_ITERS + 2, ()
-        work = [vm(*field), vm(*field), vm(NB, *field), vm(6, *block), vm(*block), vm(NY, LANES),
-                vm(40, LANES), vm(32, LANES), vm(CG_ITERS, 16, LANES), vm(NB, 16, LANES), vm(2, 16, LANES)]
+        work = [vm(*field), vm(*field), vm(NB, *field), vm(NP, ROWS, FACES, *TILE), vm(*block), vm(NY, LANES),
+                vm(40, LANES), vm(32, LANES), vm(CG_ITERS, 16, LANES), vm(NB, 16, LANES), vm(2, 16, LANES), vm(*block)]
     else:
         rounds, reds = 3, (2,)
-        work = [vm(*field), vm(*field), vm(*field), vm(*block), vm(*block), vm(6, *block), vm(*block)]
-    faces = [vm(rounds, 2, NY // 2, LANES), vm(rounds, 2, NP, 1, LANES), vm(rounds, 2, 2, 8, LANES)] * 2
+        work = [vm(*field), vm(*field), vm(*field), vm(*block), vm(*block), vm(NP, ROWS, FACES, *TILE), vm(*block)]
+    work += [vm(NP, FOLD, LANES), vm(LANES, LANES), vm(*block), vm(*block)]
+    sides = [vm(rounds, 2, FOLD, LANES), vm(rounds, 2, NP, 1, LANES)]
+    faces = sides + [vm(rounds, FOLD, LANES)] + sides + [vm(rounds, 2, FOLD, LANES)]
     rows = [vm(*reds, 3, 1, LANES)] + [vm(*reds, n, 1, LANES) for n in counts]
     dma = pltpu.SemaphoreType.DMA
     sems = [dma((6,)), dma((2,)), dma((rounds, 6)), dma((rounds, 6)), dma((*reds, 3, 8)), dma((*reds, 3, 8))]

time: 324 us -> 296 us (0.914)
  Pallas kernels: 318 us -> 290 us
    pallas_call x1, Pallas kernels: 77.8 us -> 61 us  [local_solve(): u_out, r_out, row = call(basis_kernel, 'basis', 0)(*args)]
    pallas_call x1, Pallas kernels: 240 us -> 229 us  [local_solve(): call(plain_kernel, 'plain', 1)(*args)]
where the time goes in v2:
time: 296 us
  Pallas kernels  290 us (98%)
  local copies, waits for them, and re-layouts  4.63 us (2%)
    pallas_call x1, Pallas kernels, local_solve(): call(plain_kernel, 'plain', 1)(*args)  229 us
    pallas_call x1, Pallas kernels, local_solve(): u_out, r_out, row = call(basis_kernel, 'basis', 0)(*args)  61 us

profile of v2, /device:TPU:0, one launch (start us, length us, event | category | flops | bytes accessed | tf_op | source)
XLA Modules:
  0.0 295.7 jit_solution(2441750017540377185)
XLA Ops:
  0.6 0.0 copy-start
  0.6 0.0 copy-start.1
  0.6 61.0 %basis.1 = (f32[32,64,64]{2,1,0:T(8,128)}, f32[32,64,64]{2,1,0:T(8,128)}, f32[1,128]{1,0:T(1,128)S(1)}) custom-call(f32[32,64,64]{2,1,0:T(8,128)} %k_hbm.1, f32[6,256,256]{2,1,0:T(8,128)} %g_hbm.1, f32[32,64,64]{2,1,0:T(8,128)} %f_hbm.1, f32[32,64,64]{2,1,0:T(8,128)} %u_hbm.1), custom_call_target="tpu_custom_call" | custom-call | tf_op jit(solution)/shard_map/basis/pallas_call | solution.py:730
  61.6 0.6 slice.10
  62.9 0.0 copy-done
  62.9 0.0 copy-done.1
  62.9 229.4 %conditional.1 = (f32[32,64,64]{2,1,0:T(8,128)}, f32[32,64,64]{2,1,0:T(8,128)}, f32[8]{0:T(128)S(1)}) conditional(s32[]{:T(128)} %bitcast.2, (f32[32,64,64]{2,1,0:T(8,128)S(1)}, f32[6,256,256]{2,1,0:T(8,128)S(1)}, f32[32,64,64]{2,1,0:T(8,128)}, f32[32,64,64]{2,1,0:T(8,128)}) %tuple.29, (f32[1,128]{1,0:T(1,128)S(1)}, f32[32,64,64]{2,1,0:T(8,128)}, ...), branch_computations={%region_0.0_spmd, %region_1.0_spmd} | conditional | bytes 88 | solution.py:731
  62.9 228.7 %plain.1 = (f32[32,64,64]{2,1,0:T(8,128)}, f32[32,64,64]{2,1,0:T(8,128)}, f32[1,128]{1,0:T(1,128)}) custom-call(f32[32,64,64]{2,1,0:T(8,128)S(1)} %get-tuple-element.21.k_hbm, f32[6,256,256]{2,1,0:T(8,128)S(1)} %get-tuple-element.22.g_hbm, f32[32,64,64]{2,1,0:T(8,128)} %get-tuple-element.23.f_hbm, f32[32,64,64]{2,1,0:T(8,128)} %get-tuple-element.24.u_hbm), custom_call_target="tpu_custom_call" | custom-call | tf_op jit(solution)/shard_map/cond/branch_0_fun/plain/pallas_call | solution.py:734
  291.7 0.7 slice_bitcast_fusion
  292.3 0.0 copy-start.3
  292.3 0.0 copy-start.2
  292.3 2.4 copy.15
  294.7 0.0 copy-done.2
  294.7 1.0 copy.16
  295.7 0.0 copy-done.3
Async XLA Ops:
  0.6 62.3 %copy-start = (f32[6,256,256]{2,1,0:T(8,128)S(1)}, f32[6,256,256]{2,1,0:T(8,128)}, u32[]{:S(2)}) copy-start(f32[6,256,256]{2,1,0:T(8,128)} %g_hbm.1) | copy-start | bytes 4718596
  0.6 62.3 %copy-start.1 = (f32[32,64,64]{2,1,0:T(8,128)S(1)}, f32[32,64,64]{2,1,0:T(8,128)}, u32[]{:S(2)}) copy-start(f32[32,64,64]{2,1,0:T(8,128)} %k_hbm.1) | copy-start | bytes 1572868
  292.3 3.4 %copy-start.3 = (f32[8]{0:T(128)}, f32[8]{0:T(128)S(1)}, u32[]{:S(2)}) copy-start(f32[8]{0:T(128)S(1)} %get-tuple-element.58) | copy-start | bytes 100
  292.3 2.4 copy-start.2

commit v3 on v2

--- a/solution.py
+++ b/solution.py
@@ -15,6 +15,7 @@
 MESH = pl.DeviceIdType.MESH
 AXES = ('gx', 'gy', 'gz')
 BOUND = 4096.0
+VMEM_BYTES = 60_000_000
 F32 = jnp.float32
 SUB, LANES, HALF, LOW = 8, 128, 64, 63
 ROWS = NY // SUB
@@ -78,6 +79,9 @@
             self.has.append(self.pos[axis] < counts[axis] - 1)
         (self.xs, self.ys, self.zs, self.xr, self.yr, self.zr, self.send_sem, self.recv_sem) = bufs
 
+    def neighbour(self, face):
+        return {AXES[face // 2]: self.pos[face // 2] + (1 if face % 2 else -1)}
+
     def source(self, rnd, face):
         axis, high = face // 2, face % 2
         return self.zs.at[rnd] if axis == 2 else (self.xs, self.ys)[axis].at[rnd, high]
@@ -86,11 +90,10 @@
         axis, high = face // 2, face % 2
         src = self.source(rnd, face)
         dst = (self.xr, self.yr, self.zr)[axis]
-        step = 1 if high else -1
         return pltpu.make_async_remote_copy(
             src_ref=src, dst_ref=dst.at[rnd, 1 - high],
             send_sem=self.send_sem.at[rnd, face], recv_sem=self.recv_sem.at[rnd, face ^ 1],
-            device_id={AXES[axis]: self.pos[axis] + step}, device_id_type=MESH)
+            device_id=self.neighbour(face), device_id_type=MESH)
 
     def send(self, rnd, face):
         @pl.when(self.has[face])
@@ -101,14 +104,13 @@
         axis, high = face // 2, face % 2
         src = self.source(rnd, face)
         dst = (self.xr, self.yr, self.zr)[axis]
-        step = 1 if high else -1
 
         @pl.when(self.has[face])
         def _():
             pltpu.make_async_remote_copy(
                 src_ref=src, dst_ref=dst.at[rnd, high],
                 send_sem=self.send_sem.at[rnd, face], recv_sem=self.recv_sem.at[rnd, face],
-                device_id={AXES[axis]: self.pos[axis] + step}, device_id_type=MESH).wait_recv()
+                device_id=self.neighbour(face), device_id_type=MESH).wait_recv()
 
     def wait_send(self, rnd, face):
         @pl.when(self.has[face])
@@ -116,14 +118,39 @@
             self.copies(rnd, face).wait_send()
 
 
-def barrier_all_lines(comm):
+GROUPS = (('gx',), ('gy', 'gz'))
+
+
+def group_of(comm, group):
+    sizes = [comm.counts[AXES.index(name)] for name in group]
+    size, rank = 1, 0
+    for name, n in zip(group, sizes):
+        size, rank = size * n, rank * n + comm.pos[AXES.index(name)]
+
+    def peer(off):
+        left, where = lax.rem(rank + off, size), {}
+        for name, n in reversed(tuple(zip(group, sizes))):
+            where[name], left = lax.rem(left, n), lax.div(left, n)
+        return where
+    return size, rank, peer
+
+
+def greet_faces(comm):
     sem = pltpu.get_barrier_semaphore()
-    total = 0
-    for axis in range(3):
-        n = comm.counts[axis]
-        for off in range(1, n):
-            pl.semaphore_signal(sem, inc=1, device_id={AXES[axis]: lax.rem(comm.pos[axis] + off, n)}, device_id_type=MESH)
-            total += 1
+    for face in range(FACES):
+        @pl.when(comm.has[face])
+        def _():
+            pl.semaphore_signal(sem, inc=1, device_id=comm.neighbour(face), device_id_type=MESH)
+    return sem, sum(flag.astype(jnp.int32) for flag in comm.has)
+
+
+def greet_groups(comm):
+    sem, total = pltpu.get_barrier_semaphore(), 0
+    for group in GROUPS:
+        size, _, peer = group_of(comm, group)
+        for off in range(1, size):
+            pl.semaphore_signal(sem, inc=1, device_id=peer(off), device_id_type=MESH)
+        total += size - 1
     return sem, total
 
 
@@ -131,25 +158,20 @@
     def __init__(self, comm, send_row, recv_rows, send_sem, recv_sem):
         self.comm, self.send_row, self.recv_rows, self.ss, self.rs = comm, send_row, recv_rows, send_sem, recv_sem
 
-    def copy(self, axis, off):
-        n, me = self.comm.counts[axis], self.comm.pos[axis]
-        return pltpu.make_async_remote_copy(
-            src_ref=self.send_row.at[axis], dst_ref=self.recv_rows[axis].at[me],
-            send_sem=self.ss.at[axis, off], recv_sem=self.rs.at[axis, off],
-            device_id={AXES[axis]: lax.rem(me + off, n)}, device_id_type=MESH)
-
     def run(self, row):
-        for axis in range(3):
-            n, me = self.comm.counts[axis], self.comm.pos[axis]
-            rows = self.recv_rows[axis]
-            self.send_row[axis] = row
-            rows[me] = row
-            for off in range(1, n):
-                self.copy(axis, off).start()
-            for off in range(1, n):
-                self.copy(axis, off).wait()
-            parts = [rows[i] for i in range(n)]
-            row = total_of(parts)
+        for stage, group in enumerate(GROUPS):
+            size, rank, peer = group_of(self.comm, group)
+            rows = self.recv_rows[stage]
+            self.send_row[stage] = row
+            copies = [pltpu.make_async_remote_copy(
+                src_ref=self.send_row.at[stage], dst_ref=rows.at[rank], send_sem=self.ss.at[stage, off],
+                recv_sem=self.rs.at[stage, off], device_id=peer(off), device_id_type=MESH) for off in range(1, size)]
+            for copy in copies:
+                copy.start()
+            rows[rank] = row
+            for copy in copies:
+                copy.wait()
+            row = total_of(rows[i] for i in range(size))
         return row
 
 
@@ -167,8 +189,8 @@
     comm.xs[rnd, 1] = jnp.where(lane < HALF, turn_half(a), b)
 
 
-def face_mask(turn):
-    return ((lane_iota(FOLD) + 1) & LOW) < turn
+def face_mask(turn, rows=FOLD):
+    return ((lane_iota(rows) + 1) & LOW) < turn
 
 
 def pack_z(comm, rnd, ref, tree):
@@ -177,6 +199,10 @@
         tree[p] = jnp.where(face_mask(2), low, spin(high, 2))
         return carry
     lax.fori_loop(0, NP, fold, 0, unroll=8)
+    join_z(comm, rnd, tree)
+
+
+def join_z(comm, rnd, tree):
     parts = [tree[p] for p in range(NP)]
     for turn in TURNS:
         parts = [jnp.where(face_mask(turn), parts[i], spin(parts[i + 1], turn)) for i in range(0, len(parts), 2)]
@@ -185,7 +211,7 @@
 
 def unpack_z(comm, rnd, tree):
     odd = (lane_iota(FOLD) & 1) == 1
-    parts = [jnp.where(odd, spin(comm.zr[rnd, 1], LOW), spin(comm.zr[rnd, 0], HALF + 1))]
+    parts = [jnp.where(odd, spin(comm.zr[rnd, 1], LOW - 2), spin(comm.zr[rnd, 0], HALF - 1))]
     for turn in reversed(TURNS):
         parts = [q for part in parts for q in (part, spin(part, LANES - turn))]
     for p in range(NP):
@@ -196,8 +222,8 @@
     unpack_z(comm, rnd, tree)
 
     def fold(p, carry):
-        ghost[p, 0:FOLD, :] = tree[p]
-        ghost[p, FOLD:NY, :] = spin(tree[p], LANES - 2)
+        ghost[p, 0:FOLD, :] = spin(tree[p], 2)
+        ghost[p, FOLD:NY, :] = tree[p]
         return carry
     lax.fori_loop(0, NP, fold, 0, unroll=8)
 
@@ -261,8 +287,8 @@
     return tuple(jnp.zeros(TILE, F32) for _ in range(n))
 
 
-def send_faces(comm, rnd, ref, tree):
-    pack_z(comm, rnd, ref, tree)
+def send_faces(comm, rnd, ref, tree, folded=False):
+    (join_z if folded else functools.partial(pack_z, ref=ref))(comm, rnd, tree=tree)
     for face in (4, 5):
         comm.send(rnd, face)
     pack_x_faces(comm, rnd, ref)
@@ -439,9 +465,9 @@
     return avec, cvec, ok
 
 
-def squares_row(hist_ref, full_ref, ok):
+def squares_row(hist_ref, full_ref):
     lane = lane_iota(1)
-    out = jnp.where(lane == 8, ok, 0.0)
+    out = jnp.zeros((1, LANES), F32)
     for t in range(CG_ITERS):
         cvec = hist_ref[t]
         acc = full_ref[0] * hist_ref[t, one(0)]
@@ -451,15 +477,15 @@
     return out
 
 
-def basis_kernel(counts, k_hbm, g_hbm, f_hbm, u_hbm, uo_hbm, ro_hbm, h_ref,
+def basis_kernel(counts, k_hbm, g_hbm, f_hbm, u_hbm, u_out, r_out, h_ref, ok_ref,
                  raw_k, raw_u, raw_f, slab_x, slab_y, slab_z, k_ref, u_ref, z_ref, coef_ref, d_ref, sums_ref,
                  mom_ref, pc_ref, hist_ref, full_ref, comb_ref, edge_ref, tree, square, k_ghost, u_ghost,
-                 xs, ys, zs, xr, yr, zr, send_row, rows_x, rows_y, rows_z,
-                 load_sem, store_sem, send_sem, recv_sem, red_ss, red_rs):
+                 xs, ys, zs, xr, yr, zr, send_row, rows_a, rows_b,
+                 load_sem, send_sem, recv_sem, red_ss, red_rs):
     comm = Comm(counts, (xs, ys, zs, xr, yr, zr, send_sem, recv_sem))
     raws, slabs = (raw_k, raw_u, raw_f), (slab_x, slab_y, slab_z)
     loads = start_up(comm, (k_hbm, g_hbm, f_hbm, u_hbm), raws, slabs, load_sem)
-    greet = barrier_all_lines(comm)
+    greet = greet_faces(comm)
     zero_ends(comm, range(1, CG_ITERS + 2))
     sums_ref[...] = jnp.zeros(sums_ref.shape, F32)
     for k in range(CG_ITERS):
@@ -516,16 +542,23 @@
                 term = coef_ref[plane - 1, t, face] * layer[t // 4][part]
                 ref[plane, own(t), :] = ref[plane, own(t), :] + weigh(term)
 
+        first, last = row_iota(SUB) == 0, row_iota(SUB) == SUB - 1
+
         def body(p, state):
-            for end, t, sub in ((0, 0, 0), (1, ROWS - 1, SUB - 1)):
-                row = R0 + SUB * t + sub
-                term = coef_ref[p, t, 2 + end, one(sub), :] * comm.yr[rnd, end, p]
-                ref[p + 1, one(row), :] = ref[p + 1, one(row), :] + weigh(term)
-            for i in range(2):
-                rows = slice(R0 + FOLD * i, R0 + FOLD * i + FOLD)
-                ghost = spin(tree[p], LANES - 2) if i else tree[p]
-                term = edge_ref[p, FOLD * i:FOLD * i + FOLD, :] * ghost
-                ref[p + 1, rows, :] = ref[p + 1, rows, :] + weigh(term)
+            turned = [spin(tree[p], 2), tree[p]]
+            news = []
+            for t in range(ROWS):
+                part = slice(SUB * (t % 4), SUB * (t % 4) + SUB)
+                term = edge_ref[p, tile(t), :] * turned[t // 4][part]
+                for end, at, sub, mask in ((0, 0, 0, first), (1, ROWS - 1, SUB - 1, last)):
+                    if t == at:
+                        line = coef_ref[p, t, 2 + end, one(sub), :] * comm.yr[rnd, end, p]
+                        term = term + jnp.where(mask, line, 0.0)
+                news.append(ref[p + 1, own(t), :] + weigh(term))
+                ref[p + 1, own(t), :] = news[t]
+            if k < CG_ITERS - 1:
+                for t in range(4):
+                    tree[p, tile(t), :] = jnp.where(face_mask(2, SUB), news[t], spin(news[t + 4], 2))
         sweep(body, unroll=4)
 
     for k in range(CG_ITERS):
@@ -545,12 +578,12 @@
             comm.wait_recv(rnd, face)
         late_terms(k, rnd)
         if k < CG_ITERS - 1:
-            send_faces(comm, rnd + 1, z_ref.at[k + 1], tree)
+            send_faces(comm, rnd + 1, z_ref.at[k + 1], tree, folded=True)
     products(CG_ITERS)
 
     total = jnp.broadcast_to(lane_sum(sums_ref[...]), (NY, LANES))
     row = row_sum(jnp.where(lane_iota(64) == row_iota(64), total, 0.0))
-    red = Reducer(comm, send_row, (rows_x, rows_y, rows_z), red_ss, red_rs)
+    red = Reducer(comm, send_row, (rows_a, rows_b), red_ss, red_rs)
     row = red.run(row)
     avec, cvec, ok = solve_coefficients(row, mom_ref, pc_ref, hist_ref, full_ref)
     comb_ref[0] = avec
@@ -571,35 +604,31 @@
                 rt = rt + c_co[i] * basis[i]
             ut = u_ref[p + 1, row, :] + ut
             rt = d_ref[p, rows, :] * rt
-            raw_u[p, rows, :] = ut[:, :HALF]
-            raw_u[p + NP, rows, :] = turn_half(ut)[:, :HALF]
-            raw_f[p, rows, :] = rt[:, :HALF]
-            raw_f[p + NP, rows, :] = turn_half(rt)[:, :HALF]
+            u_out[p, rows, :] = ut[:, :HALF]
+            u_out[p + NP, rows, :] = turn_half(ut)[:, :HALF]
+            r_out[p, rows, :] = rt[:, :HALF]
+            r_out[p + NP, rows, :] = turn_half(rt)[:, :HALF]
         return carry
 
     lax.fori_loop(0, NP, combine, 0)
-    outs = [pltpu.make_async_copy(raw_u, uo_hbm, store_sem.at[0]), pltpu.make_async_copy(raw_f, ro_hbm, store_sem.at[1])]
-    for out in outs:
-        out.start()
-    h_ref[...] = squares_row(hist_ref, full_ref, ok)
+    h_ref[...] = squares_row(hist_ref, full_ref)
+    ok_ref[0, 0] = ok[0, 0].astype(jnp.int32)
     for rnd in range(CG_ITERS + 2):
         for face in range(FACES):
             comm.wait_send(rnd, face)
-    for out in outs:
-        out.wait()
-
-
-def plain_kernel(counts, k_hbm, g_hbm, f_hbm, u_hbm, uo_hbm, ro_hbm, h_ref,
+
+
+def plain_kernel(counts, k_hbm, g_hbm, f_hbm, u_hbm, u_out, r_out, h_ref,
                  raw_k, raw_u, raw_f, slab_x, slab_y, slab_z, k_ref, u_ref, p_ref, q_ref, r_ref, coef_ref, d_ref, tree, square, k_ghost, u_ghost,
-                 xs, ys, zs, xr, yr, zr, send_row, rows_x, rows_y, rows_z,
-                 load_sem, store_sem, send_sem, recv_sem, red_ss, red_rs):
+                 xs, ys, zs, xr, yr, zr, send_row, rows_a, rows_b,
+                 load_sem, send_sem, recv_sem, red_ss, red_rs):
     comm = Comm(counts, (xs, ys, zs, xr, yr, zr, send_sem, recv_sem))
     raws, slabs = (raw_k, raw_u, raw_f), (slab_x, slab_y, slab_z)
     loads = start_up(comm, (k_hbm, g_hbm, f_hbm, u_hbm), raws, slabs, load_sem)
-    greet = barrier_all_lines(comm)
+    greet = greet_groups(comm)
     zero_ends(comm, range(1, 3))
     first_exchange(comm, loads, greet, raws, slabs, k_ref, u_ref, tree, square, k_ghost, u_ghost)
-    red = [Reducer(comm, send_row.at[i], (rows_x.at[i], rows_y.at[i], rows_z.at[i]), red_ss.at[i], red_rs.at[i]) for i in range(2)]
+    red = [Reducer(comm, send_row.at[i], (rows_a.at[i], rows_b.at[i]), red_ss.at[i], red_rs.at[i]) for i in range(2)]
 
     def reduce(which, accs):
         lane = lane_iota(1)
@@ -672,19 +701,14 @@
     h_ref[...] = hist
 
     def finish(p, carry):
-        write_plane(raw_u, p, u_ref[p + 1, R0:R0 + NY, :])
-        write_plane(raw_f, p, r_ref[p])
+        write_plane(u_out, p, u_ref[p + 1, R0:R0 + NY, :])
+        write_plane(r_out, p, r_ref[p])
         return carry
 
     lax.fori_loop(0, NP, finish, 0)
-    outs = [pltpu.make_async_copy(raw_u, uo_hbm, store_sem.at[0]), pltpu.make_async_copy(raw_f, ro_hbm, store_sem.at[1])]
-    for out in outs:
-        out.start()
     for rnd in range(2):
         for face in range(FACES):
             comm.wait_send(rnd, face)
-    for out in outs:
-        out.wait()
 
 
 def scratch_for(kind, counts):
@@ -702,9 +726,10 @@
     work += [vm(NP, FOLD, LANES), vm(LANES, LANES), vm(*block), vm(*block)]
     sides = [vm(rounds, 2, FOLD, LANES), vm(rounds, 2, NP, 1, LANES)]
     faces = sides + [vm(rounds, FOLD, LANES)] + sides + [vm(rounds, 2, FOLD, LANES)]
-    rows = [vm(*reds, 3, 1, LANES)] + [vm(*reds, n, 1, LANES) for n in counts]
+    sizes = [counts[0], counts[1] * counts[2]]
+    rows = [vm(*reds, 2, 1, LANES)] + [vm(*reds, n, 1, LANES) for n in sizes]
     dma = pltpu.SemaphoreType.DMA
-    sems = [dma((6,)), dma((2,)), dma((rounds, 6)), dma((rounds, 6)), dma((*reds, 3, 8)), dma((*reds, 3, 8))]
+    sems = [dma((6,)), dma((rounds, 6)), dma((rounds, 6)), dma((*reds, 2, max(sizes))), dma((*reds, 2, max(sizes)))]
     return raws + work + faces + rows + sems
 
 
@@ -713,25 +738,24 @@
     grid_spec = P(*AXES)
     block = jax.ShapeDtypeStruct((NX, NY, NZ), F32)
 
-    def call(kernel, kind, ident):
-        hbm = pl.BlockSpec(memory_space=pl.ANY)
+    def call(kernel, kind, ident, *more):
+        hbm, vmem = pl.BlockSpec(memory_space=pltpu.HBM), pl.BlockSpec(memory_space=pltpu.VMEM)
+        smem = [pl.BlockSpec(memory_space=pltpu.SMEM)] * len(more)
         return pl.pallas_call(
             functools.partial(kernel, counts),
-            out_shape=(block, block, jax.ShapeDtypeStruct((1, LANES), F32)),
+            out_shape=(block, block, jax.ShapeDtypeStruct((1, LANES), F32), *more),
             in_specs=[hbm] * 4,
-            out_specs=(hbm, hbm, pl.BlockSpec(memory_space=pltpu.VMEM)),
+            out_specs=(vmem, vmem, vmem, *smem),
             scratch_shapes=scratch_for(kind, counts),
-            compiler_params=pltpu.CompilerParams(collective_id=ident, has_side_effects=True),
+            compiler_params=pltpu.CompilerParams(collective_id=ident, has_side_effects=True, vmem_limit_bytes=VMEM_BYTES),
             name=kind,
         )
 
     def local_solve(k_cell, k_ghost, f_rhs, u_init):
         args = (k_cell, k_ghost, f_rhs, u_init)
-        u_out, r_out, row = call(basis_kernel, 'basis', 0)(*args)
-        u_out, r_out, row = lax.cond(
-            row[0, 8] > 0.5,
-            lambda: (u_out, r_out, row),
-            lambda: tuple(call(plain_kernel, 'plain', 1)(*args)))
+        *fast, ok = call(basis_kernel, 'basis', 0, jax.ShapeDtypeStruct((1, 1), jnp.int32))(*args)
+        u_out, r_out, row = lax.cond(ok[0, 0] > 0, lambda: tuple(fast),
+                                     lambda: tuple(call(plain_kernel, 'plain', 1)(*args)))
         return u_out, r_out, row[0, 0:CG_ITERS]
 
     return jax.shard_map(local_solve, mesh=mesh, in_specs=(grid_spec, P(), grid_spec, grid_spec),

time: 296 us -> 255 us (0.86)
  Pallas kernels: 290 us -> 251 us
    pallas_call x1, Pallas kernels: 229 us -> 194 us  [local_solve(): call(plain_kernel, 'plain', 1)(*args)]
    pallas_call x1, Pallas kernels: 61 us -> 57 us  [local_solve(): call(basis_kernel, 'basis', 0, jax.ShapeDtypeStruct((1, 1), jnp.int32))]
where the time goes in v3:
time: 255 us
  Pallas kernels  251 us (98%)
  local copies, waits for them, and re-layouts  2.62 us (1%)
    pallas_call x1, Pallas kernels, local_solve(): call(plain_kernel, 'plain', 1)(*args)  194 us
    pallas_call x1, Pallas kernels, local_solve(): call(basis_kernel, 'basis', 0, jax.ShapeDtypeStruct((1, 1), jnp.int32))  57 us

profile of v3, /device:TPU:0, one launch (start us, length us, event | category | flops | bytes accessed | tf_op | source)
XLA Modules:
  0.0 254.9 jit_solution(6846220607229391650)
XLA Ops:
  0.6 0.0 copy-start
  0.6 0.0 copy-start.1
  0.7 0.0 copy-start.2
  0.7 0.0 copy-start.3
  0.7 57.0 %basis.1 = (f32[32,64,64]{2,1,0:T(8,128)S(1)}, f32[32,64,64]{2,1,0:T(8,128)S(1)}, f32[1,128]{1,0:T(1,128)S(1)}, s32[1,1]{1,0:T(1,128)}) custom-call(f32[32,64,64]{2,1,0:T(8,128)} %k_hbm.1, f32[6,256,256]{2,1,0:T(8,128)} %g_hbm.1, f32[32,64,64]{2,1,0:T(8,128)} %f_hbm.1, f32[32,64,64]{2,1,0:T(8,128)} %u_hbm.1), custom_call_target="tpu_custom_call" | custom-call | tf_op jit(solution)/shard_map/basis/pallas_call | solution.py:756
  58.3 0.0 copy-done
  58.3 0.0 copy-done.1
  58.4 0.0 copy-done.2
  58.4 0.0 copy-done.3
  58.4 194.6 %conditional.1 = (f32[32,64,64]{2,1,0:T(8,128)S(1)}, f32[32,64,64]{2,1,0:T(8,128)S(1)}, f32[8]{0:T(128)S(1)}) conditional(s32[]{:T(128)} %bitcast.2, (f32[32,64,64]{2,1,0:T(8,128)S(1)}, f32[6,256,256]{2,1,0:T(8,128)S(1)}, f32[32,64,64]{2,1,0:T(8,128)S(1)}, f32[32,64,64]{2,1,0:T(8,128)S(1)}) %tuple.31, (f32[1,128]{1,0:T(1,128)S(1)}, ...), branch_computations={%region_0.0_spmd, %region_1.0_spmd} | conditional | bytes 88 | solution.py:757
  58.4 193.9 %plain.1 = (f32[32,64,64]{2,1,0:T(8,128)S(1)}, f32[32,64,64]{2,1,0:T(8,128)S(1)}, f32[1,128]{1,0:T(1,128)}) custom-call(f32[32,64,64]{2,1,0:T(8,128)S(1)} %get-tuple-element.21.k_hbm, f32[6,256,256]{2,1,0:T(8,128)S(1)} %get-tuple-element.22.g_hbm, f32[32,64,64]{2,1,0:T(8,128)S(1)} %get-tuple-element.23.f_hbm, f32[32,64,64]{2,1,0:T(8,128)S(1)} %get-tuple-element.24.u_hbm), custom_call_target="tpu_custom_call" | custom-call | tf_op jit(solution)/shard_map/cond/branch_0_fun/plain/pallas_call | solution.py:758
  252.3 0.7 slice_bitcast_fusion
  252.9 0.0 copy-start.4
  252.9 1.0 copy.15
  253.9 1.0 copy.16
  254.9 0.0 copy-done.4
Async XLA Ops:
  0.6 57.7 %copy-start = (f32[6,256,256]{2,1,0:T(8,128)S(1)}, f32[6,256,256]{2,1,0:T(8,128)}, u32[]{:S(2)}) copy-start(f32[6,256,256]{2,1,0:T(8,128)} %g_hbm.1) | copy-start | bytes 4718596
  0.6 57.7 %copy-start.1 = (f32[32,64,64]{2,1,0:T(8,128)S(1)}, f32[32,64,64]{2,1,0:T(8,128)}, u32[]{:S(2)}) copy-start(f32[32,64,64]{2,1,0:T(8,128)} %k_hbm.1) | copy-start | bytes 1572868
  0.7 57.7 %copy-start.2 = (f32[32,64,64]{2,1,0:T(8,128)S(1)}, f32[32,64,64]{2,1,0:T(8,128)}, u32[]{:S(2)}) copy-start(f32[32,64,64]{2,1,0:T(8,128)} %f_hbm.1) | copy-start | bytes 1572868
  0.7 57.7 %copy-start.3 = (f32[32,64,64]{2,1,0:T(8,128)S(1)}, f32[32,64,64]{2,1,0:T(8,128)}, u32[]{:S(2)}) copy-start(f32[32,64,64]{2,1,0:T(8,128)} %u_hbm.1) | copy-start | bytes 1572868
  252.9 1.9 copy-start.4

commit v4 on v3

--- a/solution.py
+++ b/solution.py
@@ -15,6 +15,7 @@
 MESH = pl.DeviceIdType.MESH
 AXES = ('gx', 'gy', 'gz')
 BOUND = 4096.0
+GRAM = 2 * NB
 VMEM_BYTES = 60_000_000
 F32 = jnp.float32
 SUB, LANES, HALF, LOW = 8, 128, 64, 63
@@ -198,7 +199,7 @@
         low, high = ref[p + 1, R0:R0 + FOLD, :], ref[p + 1, R0 + FOLD:R0 + NY, :]
         tree[p] = jnp.where(face_mask(2), low, spin(high, 2))
         return carry
-    lax.fori_loop(0, NP, fold, 0, unroll=8)
+    lax.fori_loop(0, NP, fold, 0, unroll=NP)
     join_z(comm, rnd, tree)
 
 
@@ -225,7 +226,7 @@
         ghost[p, 0:FOLD, :] = spin(tree[p], 2)
         ghost[p, FOLD:NY, :] = tree[p]
         return carry
-    lax.fori_loop(0, NP, fold, 0, unroll=8)
+    lax.fori_loop(0, NP, fold, 0, unroll=NP)
 
 
 def inner_planes(ref):
@@ -301,7 +302,7 @@
 def load_field(raw, ref):
     def body(p, state):
         ref[p + 1, R0:R0 + NY, :] = jnp.concatenate([raw[p], raw[p + NP]], axis=1)
-    sweep(body, unroll=4)
+    sweep(body, unroll=NP)
 
 
 def fill_ghost_conductivity(comm, square, gx_slab, gy_slab, gz_slab):
@@ -341,8 +342,11 @@
         @pl.when(jnp.logical_not(comm.has[face]))
         def _():
             buf = (comm.xr, comm.yr, comm.zr)[face // 2]
-            for rnd in rounds:
+
+            def clear(rnd, carry):
                 buf[rnd, face % 2] = jnp.zeros(buf.shape[2:], F32)
+                return carry
+            lax.fori_loop(1, rounds, clear, 0)
 
 
 def lanes_of(pos):
@@ -415,7 +419,7 @@
 def solve_coefficients(row, mom_ref, pc_ref, hist_ref, full_ref):
     lane24, line24 = lane_iota(24), row_iota(24)
     wide = jnp.broadcast_to(row, (24, LANES))
-    base = lane_sum(jnp.where((lane24 == line24) & (lane24 < 17), wide, 0.0))
+    base = lane_sum(jnp.where((lane24 == line24 + 1) & (line24 < 17), wide, 0.0))
     base = jnp.broadcast_to(base, (24, LANES))
     first, second = base[0:1], base[1:2]
     even = (line24 & 1) == 0
@@ -426,7 +430,7 @@
     for k in range(NB):
         big = jnp.maximum(line16, k)
         small = jnp.minimum(line16, k)
-        want = 17 + lax.shift_right_logical(big * (big + 1), 1) + small
+        want = GRAM + NB * big + small
         col = lane_sum(jnp.where((lane16 == want) & (line16 < NB), wide, 0.0))
         full_ref[k] = jnp.broadcast_to(col, WIDE)
     zeros8 = jnp.zeros(TILE, F32)
@@ -479,17 +483,24 @@
 
 def basis_kernel(counts, k_hbm, g_hbm, f_hbm, u_hbm, u_out, r_out, h_ref, ok_ref,
                  raw_k, raw_u, raw_f, slab_x, slab_y, slab_z, k_ref, u_ref, z_ref, coef_ref, d_ref, sums_ref,
-                 mom_ref, pc_ref, hist_ref, full_ref, comb_ref, edge_ref, tree, square, k_ghost, u_ghost,
+                 mom_ref, pc_ref, hist_ref, full_ref, comb_ref, edge_ref, part_ref, tree, square, k_ghost, u_ghost,
                  xs, ys, zs, xr, yr, zr, send_row, rows_a, rows_b,
                  load_sem, send_sem, recv_sem, red_ss, red_rs):
     comm = Comm(counts, (xs, ys, zs, xr, yr, zr, send_sem, recv_sem))
     raws, slabs = (raw_k, raw_u, raw_f), (slab_x, slab_y, slab_z)
     loads = start_up(comm, (k_hbm, g_hbm, f_hbm, u_hbm), raws, slabs, load_sem)
     greet = greet_faces(comm)
-    zero_ends(comm, range(1, CG_ITERS + 2))
+    zero_ends(comm, CG_ITERS + 2)
     sums_ref[...] = jnp.zeros(sums_ref.shape, F32)
-    for k in range(CG_ITERS):
-        blank_rows(z_ref.at[k])
+
+    def blank(k, carry):
+        blank_rows(z_ref.at[k + 1])
+        return carry
+    lax.fori_loop(0, CG_ITERS, blank, 0)
+
+    def nothing(p, state):
+        z_ref[0, p + 1, R0:R0 + NY, :] = jnp.zeros((NY, LANES), F32)
+    sweep(nothing, unroll=4)
     first_exchange(comm, loads, greet, raws, slabs, k_ref, u_ref, tree, square, k_ghost, u_ghost)
 
     def first(p, state):
@@ -503,44 +514,39 @@
             scaled[4:] = jnp.where(lane == 0, 0.0, low), jnp.where(lane == LOW, 0.0, high)
             for i in range(FACES):
                 coef_ref[p, t, i] = scaled[i]
-            z_ref[0, p + 1, own(t), :] = resid * inv
-
-    sweep(first)
-    send_faces(comm, 2, z_ref.at[0], tree)
+            z_ref[1, p + 1, own(t), :] = resid * inv
+
+    sweep(first, unroll=4)
+    send_faces(comm, 2, z_ref.at[1], tree)
 
     def products(k):
         def body(p, accs):
-            accs = list(accs)
             for t in range(ROWS):
-                row = own(t)
                 d = d_ref[p, tile(t), :]
-                z_k = z_ref[k, p + 1, row, :]
+                z_k = z_ref[k + 1, p + 1, own(t), :]
                 dz = d * z_k
                 ddz = d * dz
-                for i in range(k + 1):
-                    z_i = z_ref[i, p + 1, row, :]
-                    accs[i] = accs[i] + ddz * z_i
-                    if i >= k - 1:
-                        accs[k + 1 + (k - i)] = accs[k + 1 + (k - i)] + dz * z_i
-            return tuple(accs)
-        accs = lax.fori_loop(0, NP, body, zero_tiles(k + 2 + (1 if k else 0)))
-        for i in range(k + 1):
-            at = 17 + k * (k + 1) // 2 + i
-            sums_ref[one(at)] = row_sum(accs[i])
-        sums_ref[one(2 * k)] = row_sum(accs[k + 1])
-        if k:
-            sums_ref[one(2 * k - 1)] = row_sum(accs[k + 2])
+                for i in range(NB):
+                    accs[i] = accs[i] + ddz * z_ref[i + 1, p + 1, own(t), :]
+                accs[NB] = accs[NB] + dz * z_k
+                accs[NB + 1] = accs[NB + 1] + dz * z_ref[k, p + 1, own(t), :]
+        accs = sweep(body, zero_tiles(NB + 2))
+        rows = [GRAM + NB * k + i for i in range(NB)] + [2 * k + 1, 2 * k]
+        for row, acc in zip(rows, accs):
+            sums_ref[pl.ds(row, 1), :] = row_sum(acc)
+
+    def weight(k):
+        return jnp.where(k == 0, 0.5, 1.0)
 
     def late_terms(k, rnd):
-        ref = z_ref.at[k + 1]
-        weigh = (lambda term: 0.5 * term) if k == 0 else (lambda term: term)
+        ref, factor = z_ref.at[k + 2], weight(k)
         unpack_z(comm, rnd, tree)
         below, above = x_ghosts(comm, rnd)
         for t in range(ROWS):
             part = slice(SUB * (t % 4), SUB * (t % 4) + SUB)
             for plane, face, layer in ((1, 0, below), (NP, 1, above)):
                 term = coef_ref[plane - 1, t, face] * layer[t // 4][part]
-                ref[plane, own(t), :] = ref[plane, own(t), :] + weigh(term)
+                part_ref[plane - 1, tile(t), :] = part_ref[plane - 1, tile(t), :] + factor * term
 
         first, last = row_iota(SUB) == 0, row_iota(SUB) == SUB - 1
 
@@ -554,35 +560,39 @@
                     if t == at:
                         line = coef_ref[p, t, 2 + end, one(sub), :] * comm.yr[rnd, end, p]
                         term = term + jnp.where(mask, line, 0.0)
-                news.append(ref[p + 1, own(t), :] + weigh(term))
+                news.append(part_ref[p, tile(t), :] + factor * term)
                 ref[p + 1, own(t), :] = news[t]
-            if k < CG_ITERS - 1:
-                for t in range(4):
-                    tree[p, tile(t), :] = jnp.where(face_mask(2, SUB), news[t], spin(news[t + 4], 2))
-        sweep(body, unroll=4)
-
-    for k in range(CG_ITERS):
-        rnd = 2 + k
-        inner_planes(z_ref.at[k])
+            for t in range(4):
+                tree[p, tile(t), :] = jnp.where(face_mask(2, SUB), news[t], spin(news[t + 4], 2))
+        sweep(body, unroll=NP)
+
+    def apply(k, carry):
+        rnd, factor = k + 2, weight(k)
+        ref = z_ref.at[k + 1]
+        inner_planes(ref)
 
         def step(p, state):
             for t in range(ROWS):
-                _, others = neighbours(z_ref.at[k], p, t)
+                _, others = neighbours(ref, p, t)
                 total = total_of(coef_ref[p, t, i] * others[i] for i in range(FACES))
-                z_new = 0.5 * total if k == 0 else total - z_ref[k - 1, p + 1, own(t), :]
-                z_ref[k + 1, p + 1, own(t), :] = z_new
+                part_ref[p, tile(t), :] = factor * total - z_ref[k, p + 1, own(t), :]
 
         sweep(step)
         products(k)
         for face in range(FACES):
             comm.wait_recv(rnd, face)
         late_terms(k, rnd)
-        if k < CG_ITERS - 1:
-            send_faces(comm, rnd + 1, z_ref.at[k + 1], tree, folded=True)
+
+        @pl.when(k < CG_ITERS - 1)
+        def _():
+            send_faces(comm, rnd + 1, z_ref.at[k + 2], tree, folded=True)
+        return carry
+
+    lax.fori_loop(0, CG_ITERS, apply, 0)
     products(CG_ITERS)
 
-    total = jnp.broadcast_to(lane_sum(sums_ref[...]), (NY, LANES))
-    row = row_sum(jnp.where(lane_iota(64) == row_iota(64), total, 0.0))
+    total = jnp.broadcast_to(lane_sum(sums_ref[...]), (LANES, LANES))
+    row = row_sum(jnp.where(lane_iota(LANES) == row_iota(LANES), total, 0.0))
     red = Reducer(comm, send_row, (rows_a, rows_b), red_ss, red_rs)
     row = red.run(row)
     avec, cvec, ok = solve_coefficients(row, mom_ref, pc_ref, hist_ref, full_ref)
@@ -596,7 +606,7 @@
         for t in range(ROWS):
             row = own(t)
             rows = tile(t)
-            basis = [z_ref[i, p + 1, row, :] for i in range(NB)]
+            basis = [z_ref[i + 1, p + 1, row, :] for i in range(NB)]
             ut, rt = a_co[0] * basis[0], c_co[0] * basis[0]
             for i in range(1, NB):
                 if i < CG_ITERS:
@@ -610,12 +620,15 @@
             r_out[p + NP, rows, :] = turn_half(rt)[:, :HALF]
         return carry
 
-    lax.fori_loop(0, NP, combine, 0)
+    lax.fori_loop(0, NP, combine, 0, unroll=4)
     h_ref[...] = squares_row(hist_ref, full_ref)
     ok_ref[0, 0] = ok[0, 0].astype(jnp.int32)
-    for rnd in range(CG_ITERS + 2):
+
+    def drain(rnd, carry):
         for face in range(FACES):
             comm.wait_send(rnd, face)
+        return carry
+    lax.fori_loop(0, CG_ITERS + 2, drain, 0)
 
 
 def plain_kernel(counts, k_hbm, g_hbm, f_hbm, u_hbm, u_out, r_out, h_ref,
@@ -626,7 +639,7 @@
     raws, slabs = (raw_k, raw_u, raw_f), (slab_x, slab_y, slab_z)
     loads = start_up(comm, (k_hbm, g_hbm, f_hbm, u_hbm), raws, slabs, load_sem)
     greet = greet_groups(comm)
-    zero_ends(comm, range(1, 3))
+    zero_ends(comm, 3)
     first_exchange(comm, loads, greet, raws, slabs, k_ref, u_ref, tree, square, k_ghost, u_ghost)
     red = [Reducer(comm, send_row.at[i], (rows_a.at[i], rows_b.at[i]), red_ss.at[i], red_rs.at[i]) for i in range(2)]
 
@@ -718,8 +731,8 @@
     raws = [vm(NX, NY, NZ)] * 3 + [vm(NY, LANES), vm(NX, LANES), vm(NX, LANES)]
     if kind == 'basis':
         rounds, reds = CG_ITERS + 2, ()
-        work = [vm(*field), vm(*field), vm(NB, *field), vm(NP, ROWS, FACES, *TILE), vm(*block), vm(NY, LANES),
-                vm(40, LANES), vm(32, LANES), vm(CG_ITERS, 16, LANES), vm(NB, 16, LANES), vm(2, 16, LANES), vm(*block)]
+        work = [vm(*field), vm(*field), vm(NB + 1, *field), vm(NP, ROWS, FACES, *TILE), vm(*block), vm(LANES, LANES),
+                vm(40, LANES), vm(32, LANES), vm(CG_ITERS, 16, LANES), vm(NB, 16, LANES), vm(2, 16, LANES), vm(*block), vm(*block)]
     else:
         rounds, reds = 3, (2,)
         work = [vm(*field), vm(*field), vm(*field), vm(*block), vm(*block), vm(NP, ROWS, FACES, *TILE), vm(*block)]

time: 255 us -> 247 us (0.969)
  Pallas kernels: 251 us -> 243 us
    pallas_call x1, Pallas kernels: 57 us -> 52.2 us  [local_solve(): call(basis_kernel, 'basis', 0, jax.ShapeDtypeStruct((1, 1), jnp.int32))]
    pallas_call x1, Pallas kernels: 194 us -> 191 us  [local_solve(): call(plain_kernel, 'plain', 1)(*args)]
where the time goes in v4:
time: 247 us
  Pallas kernels  243 us (98%)
  local copies, waits for them, and re-layouts  2.62 us (1%)
    pallas_call x1, Pallas kernels, local_solve(): call(plain_kernel, 'plain', 1)(*args)  191 us
    pallas_call x1, Pallas kernels, local_solve(): call(basis_kernel, 'basis', 0, jax.ShapeDtypeStruct((1, 1), jnp.int32))  52.2 us

profile of v4, /device:TPU:0, one launch (start us, length us, event | category | flops | bytes accessed | tf_op | source)
XLA Modules:
  0.0 247.1 jit_solution(4644735126550087203)
XLA Ops:
  0.6 0.0 copy-start
  0.6 0.0 copy-start.1
  0.7 0.0 copy-start.2
  0.7 0.0 copy-start.3
  0.7 52.2 %basis.1 = (f32[32,64,64]{2,1,0:T(8,128)S(1)}, f32[32,64,64]{2,1,0:T(8,128)S(1)}, f32[1,128]{1,0:T(1,128)S(1)}, s32[1,1]{1,0:T(1,128)}) custom-call(f32[32,64,64]{2,1,0:T(8,128)} %k_hbm.1, f32[6,256,256]{2,1,0:T(8,128)} %g_hbm.1, f32[32,64,64]{2,1,0:T(8,128)} %f_hbm.1, f32[32,64,64]{2,1,0:T(8,128)} %u_hbm.1), custom_call_target="tpu_custom_call" | custom-call | tf_op jit(solution)/shard_map/basis/pallas_call | solution.py:769
  53.5 0.0 copy-done
  53.5 0.0 copy-done.1
  53.6 0.0 copy-done.2
  53.6 0.0 copy-done.3
  53.6 191.6 %conditional.1 = (f32[32,64,64]{2,1,0:T(8,128)S(1)}, f32[32,64,64]{2,1,0:T(8,128)S(1)}, f32[8]{0:T(128)S(1)}) conditional(s32[]{:T(128)} %bitcast.2, (f32[32,64,64]{2,1,0:T(8,128)S(1)}, f32[6,256,256]{2,1,0:T(8,128)S(1)}, f32[32,64,64]{2,1,0:T(8,128)S(1)}, f32[32,64,64]{2,1,0:T(8,128)S(1)}) %tuple.31, (f32[1,128]{1,0:T(1,128)S(1)}, ...), branch_computations={%region_0.0_spmd, %region_1.0_spmd} | conditional | bytes 88 | solution.py:770
  53.6 190.9 %plain.1 = (f32[32,64,64]{2,1,0:T(8,128)S(1)}, f32[32,64,64]{2,1,0:T(8,128)S(1)}, f32[1,128]{1,0:T(1,128)}) custom-call(f32[32,64,64]{2,1,0:T(8,128)S(1)} %get-tuple-element.21.k_hbm, f32[6,256,256]{2,1,0:T(8,128)S(1)} %get-tuple-element.22.g_hbm, f32[32,64,64]{2,1,0:T(8,128)S(1)} %get-tuple-element.23.f_hbm, f32[32,64,64]{2,1,0:T(8,128)S(1)} %get-tuple-element.24.u_hbm), custom_call_target="tpu_custom_call" | custom-call | tf_op jit(solution)/shard_map/cond/branch_0_fun/plain/pallas_call | solution.py:771
  244.5 0.7 slice_bitcast_fusion
  245.2 0.0 copy-start.4
  245.2 1.0 copy.15
  246.2 1.0 copy.16
  247.1 0.0 copy-done.4
Async XLA Ops:
  0.6 52.9 %copy-start = (f32[6,256,256]{2,1,0:T(8,128)S(1)}, f32[6,256,256]{2,1,0:T(8,128)}, u32[]{:S(2)}) copy-start(f32[6,256,256]{2,1,0:T(8,128)} %g_hbm.1) | copy-start | bytes 4718596
  0.6 52.9 %copy-start.1 = (f32[32,64,64]{2,1,0:T(8,128)S(1)}, f32[32,64,64]{2,1,0:T(8,128)}, u32[]{:S(2)}) copy-start(f32[32,64,64]{2,1,0:T(8,128)} %k_hbm.1) | copy-start | bytes 1572868
  0.7 52.9 %copy-start.2 = (f32[32,64,64]{2,1,0:T(8,128)S(1)}, f32[32,64,64]{2,1,0:T(8,128)}, u32[]{:S(2)}) copy-start(f32[32,64,64]{2,1,0:T(8,128)} %f_hbm.1) | copy-start | bytes 1572868
  0.7 52.9 %copy-start.3 = (f32[32,64,64]{2,1,0:T(8,128)S(1)}, f32[32,64,64]{2,1,0:T(8,128)}, u32[]{:S(2)}) copy-start(f32[32,64,64]{2,1,0:T(8,128)} %u_hbm.1) | copy-start | bytes 1572868
  245.2 1.9 copy-start.4

commit v5 on v4

--- a/solution.py
+++ b/solution.py
@@ -724,6 +724,14 @@
             comm.wait_send(rnd, face)
 
 
+def finish_kernel(u_in, r_in, u_hbm, r_hbm, sems):
+    copies = [pltpu.make_async_copy(u_in, u_hbm, sems.at[0]), pltpu.make_async_copy(r_in, r_hbm, sems.at[1])]
+    for copy in copies:
+        copy.start()
+    for copy in copies:
+        copy.wait()
+
+
 def scratch_for(kind, counts):
     field = (NP + 2, NY + 16, LANES)
     block = (NP, NY, LANES)
@@ -769,6 +777,15 @@
         *fast, ok = call(basis_kernel, 'basis', 0, jax.ShapeDtypeStruct((1, 1), jnp.int32))(*args)
         u_out, r_out, row = lax.cond(ok[0, 0] > 0, lambda: tuple(fast),
                                      lambda: tuple(call(plain_kernel, 'plain', 1)(*args)))
+        u_out, r_out = pl.pallas_call(
+            finish_kernel,
+            out_shape=(block, block),
+            in_specs=[pl.BlockSpec(memory_space=pltpu.VMEM)] * 2,
+            out_specs=(pl.BlockSpec(memory_space=pltpu.HBM),) * 2,
+            scratch_shapes=[pltpu.SemaphoreType.DMA((2,))],
+            compiler_params=pltpu.CompilerParams(vmem_limit_bytes=VMEM_BYTES),
+            name='finish',
+        )(u_out, r_out)
         return u_out, r_out, row[0, 0:CG_ITERS]
 
     return jax.shard_map(local_solve, mesh=mesh, in_specs=(grid_spec, P(), grid_spec, grid_spec),

time: 247 us -> 247 us (level)
  no operation moved by 1% of the time
where the time goes in v5:
time: 247 us; the launch traced here: 246 us
  Pallas kernels  244 us (99%)
    pallas_call x1, Pallas kernels, local_solve(): call(plain_kernel, 'plain', 1)(*args)  191 us
    pallas_call x1, Pallas kernels, local_solve(): call(basis_kernel, 'basis', 0, jax.ShapeDtypeStruct((1, 1), jnp.int32))  52.2 us

profile of v5, /device:TPU:0, one launch (start us, length us, event | category | flops | bytes accessed | tf_op | source)
XLA Modules:
  0.0 246.5 jit_solution(16287990121497109199)
XLA Ops:
  0.6 0.0 copy-start
  0.6 0.0 copy-start.1
  0.7 0.0 copy-start.2
  0.7 0.0 copy-start.3
  0.7 52.2 %basis.1 = (f32[32,64,64]{2,1,0:T(8,128)S(1)}, f32[32,64,64]{2,1,0:T(8,128)S(1)}, f32[1,128]{1,0:T(1,128)S(1)}, s32[1,1]{1,0:T(1,128)}) custom-call(f32[32,64,64]{2,1,0:T(8,128)} %k_hbm.1, f32[6,256,256]{2,1,0:T(8,128)} %g_hbm.1, f32[32,64,64]{2,1,0:T(8,128)} %f_hbm.1, f32[32,64,64]{2,1,0:T(8,128)} %u_hbm.1), custom_call_target="tpu_custom_call" | custom-call | tf_op jit(solution)/shard_map/basis/pallas_call | solution.py:777
  53.5 0.0 copy-done
  53.6 0.0 copy-done.1
  53.6 0.0 copy-done.2
  53.6 0.0 copy-done.3
  53.6 191.6 %conditional.1 = (f32[32,64,64]{2,1,0:T(8,128)S(1)}, f32[32,64,64]{2,1,0:T(8,128)S(1)}, f32[8]{0:T(128)S(1)}) conditional(s32[]{:T(128)} %bitcast.2, (f32[32,64,64]{2,1,0:T(8,128)S(1)}, f32[6,256,256]{2,1,0:T(8,128)S(1)}, f32[32,64,64]{2,1,0:T(8,128)S(1)}, f32[32,64,64]{2,1,0:T(8,128)S(1)}) %tuple.31, (f32[1,128]{1,0:T(1,128)S(1)}, ...), branch_computations={%region_0.0_spmd, %region_1.0_spmd} | conditional | bytes 88 | solution.py:778
  53.6 190.9 %plain.1 = (f32[32,64,64]{2,1,0:T(8,128)S(1)}, f32[32,64,64]{2,1,0:T(8,128)S(1)}, f32[1,128]{1,0:T(1,128)}) custom-call(f32[32,64,64]{2,1,0:T(8,128)S(1)} %get-tuple-element.21.k_hbm, f32[6,256,256]{2,1,0:T(8,128)S(1)} %get-tuple-element.22.g_hbm, f32[32,64,64]{2,1,0:T(8,128)S(1)} %get-tuple-element.23.f_hbm, f32[32,64,64]{2,1,0:T(8,128)S(1)} %get-tuple-element.24.u_hbm), custom_call_target="tpu_custom_call" | custom-call | tf_op jit(solution)/shard_map/cond/branch_0_fun/plain/pallas_call | solution.py:779
  244.5 0.6 slice_bitcast_fusion
  245.1 0.0 copy-start.4
  245.1 1.3 finish.1
  246.5 0.0 copy-done.4
Async XLA Ops:
  0.6 52.9 %copy-start = (f32[6,256,256]{2,1,0:T(8,128)S(1)}, f32[6,256,256]{2,1,0:T(8,128)}, u32[]{:S(2)}) copy-start(f32[6,256,256]{2,1,0:T(8,128)} %g_hbm.1) | copy-start | bytes 4718596
  0.6 52.9 %copy-start.1 = (f32[32,64,64]{2,1,0:T(8,128)S(1)}, f32[32,64,64]{2,1,0:T(8,128)}, u32[]{:S(2)}) copy-start(f32[32,64,64]{2,1,0:T(8,128)} %k_hbm.1) | copy-start | bytes 1572868
  0.7 52.9 %copy-start.2 = (f32[32,64,64]{2,1,0:T(8,128)S(1)}, f32[32,64,64]{2,1,0:T(8,128)}, u32[]{:S(2)}) copy-start(f32[32,64,64]{2,1,0:T(8,128)} %f_hbm.1) | copy-start | bytes 1572868
  0.7 52.9 %copy-start.3 = (f32[32,64,64]{2,1,0:T(8,128)S(1)}, f32[32,64,64]{2,1,0:T(8,128)}, u32[]{:S(2)}) copy-start(f32[32,64,64]{2,1,0:T(8,128)} %u_hbm.1) | copy-start | bytes 1572868
  245.1 1.3 copy-start.4

commit v6 on v5

--- a/solution.py
+++ b/solution.py
@@ -24,7 +24,7 @@
 WIDE = (2 * SUB, LANES)
 FACES = 6
 FOLD = NY // 2
-TURNS = (4, 8, 16, 32)
+TURNS = ((4, 8, 12), (16, 32, 48))
 
 
 def own(t):
@@ -85,7 +85,7 @@
 
     def source(self, rnd, face):
         axis, high = face // 2, face % 2
-        return self.zs.at[rnd] if axis == 2 else (self.xs, self.ys)[axis].at[rnd, high]
+        return (self.xs, self.ys, self.zs)[axis].at[rnd, high]
 
     def copies(self, rnd, face):
         axis, high = face // 2, face % 2
@@ -205,16 +205,29 @@
 
 def join_z(comm, rnd, tree):
     parts = [tree[p] for p in range(NP)]
-    for turn in TURNS:
-        parts = [jnp.where(face_mask(turn), parts[i], spin(parts[i + 1], turn)) for i in range(0, len(parts), 2)]
-    comm.zs[rnd] = parts[0]
+    for turns in TURNS:
+        merged = []
+        for i in range(0, NP, 4)[:len(parts) // 4]:
+            out = spin(parts[i + 3], turns[-1])
+            for n in (2, 1):
+                out = jnp.where(face_mask(turns[n]), spin(parts[i + n], turns[n - 1]), out)
+            merged.append(jnp.where(face_mask(turns[0]), parts[i], out))
+        parts = merged
+    for end in range(2):
+        comm.zs[rnd, end] = halve_z(parts[0], 1 - end)
+
+
+def halve_z(packed, keep):
+    even = (lane_iota(NP) & 1) == 1 - keep
+    return jnp.where(even, packed[:NP], spin(packed[NP:], 1 if keep else LANES - 1))
 
 
 def unpack_z(comm, rnd, tree):
-    odd = (lane_iota(FOLD) & 1) == 1
-    parts = [jnp.where(odd, spin(comm.zr[rnd, 1], LOW - 2), spin(comm.zr[rnd, 0], HALF - 1))]
-    for turn in reversed(TURNS):
-        parts = [q for part in parts for q in (part, spin(part, LANES - turn))]
+    odd = (lane_iota(NP) & 1) == 1
+    low, high = comm.zr[rnd, 0], comm.zr[rnd, 1]
+    parts = [jnp.concatenate([jnp.where(odd, spin(high, LOW - 2 - i), spin(low, LOW + i)) for i in range(2)], axis=0)]
+    for turns in reversed(TURNS):
+        parts = [q for part in parts for q in (part, *(spin(part, LANES - turn) for turn in turns))]
     for p in range(NP):
         tree[p] = parts[p]
 
@@ -289,13 +302,16 @@
 
 
 def send_faces(comm, rnd, ref, tree, folded=False):
+    if not folded:
+        for p in range(NP):
+            store_plane_faces(comm, rnd, ref, p)
+    for face in (2, 3):
+        comm.send(rnd, face)
     (join_z if folded else functools.partial(pack_z, ref=ref))(comm, rnd, tree=tree)
     for face in (4, 5):
         comm.send(rnd, face)
     pack_x_faces(comm, rnd, ref)
-    for p in range(NP):
-        store_plane_faces(comm, rnd, ref, p)
-    for face in range(4):
+    for face in (0, 1):
         comm.send(rnd, face)
 
 
@@ -334,7 +350,7 @@
                     square[one((4 * (x % NP) + 2 * c + HALF * (x // NP) + shift) % LANES)] = cols[one(x)]
             turned = square[...].T
             second = ((lane_iota(FOLD) - shift) & 3) == 2
-            comm.zr[0, end] = jnp.where(second, turned[FOLD:NY], turned[:FOLD])
+            comm.zr[0, end] = halve_z(jnp.where(second, turned[FOLD:NY], turned[:FOLD]), end)
 
 
 def zero_ends(comm, rounds):
@@ -538,16 +554,18 @@
     def weight(k):
         return jnp.where(k == 0, 0.5, 1.0)
 
+    def x_terms(k, rnd):
+        factor = weight(k)
+        below, above = x_ghosts(comm, rnd)
+        for t in range(ROWS):
+            part = slice(SUB * (t % 4), SUB * (t % 4) + SUB)
+            for plane, face, layer in ((0, 0, below), (NP - 1, 1, above)):
+                term = coef_ref[plane, t, face] * layer[t // 4][part]
+                part_ref[plane, tile(t), :] = part_ref[plane, tile(t), :] + factor * term
+
     def late_terms(k, rnd):
         ref, factor = z_ref.at[k + 2], weight(k)
         unpack_z(comm, rnd, tree)
-        below, above = x_ghosts(comm, rnd)
-        for t in range(ROWS):
-            part = slice(SUB * (t % 4), SUB * (t % 4) + SUB)
-            for plane, face, layer in ((1, 0, below), (NP, 1, above)):
-                term = coef_ref[plane - 1, t, face] * layer[t // 4][part]
-                part_ref[plane - 1, tile(t), :] = part_ref[plane - 1, tile(t), :] + factor * term
-
         first, last = row_iota(SUB) == 0, row_iota(SUB) == SUB - 1
 
         def body(p, state):
@@ -562,6 +580,8 @@
                         term = term + jnp.where(mask, line, 0.0)
                 news.append(part_ref[p, tile(t), :] + factor * term)
                 ref[p + 1, own(t), :] = news[t]
+            comm.ys[rnd + 1, 0, p] = news[0][:1]
+            comm.ys[rnd + 1, 1, p] = news[ROWS - 1][SUB - 1:]
             for t in range(4):
                 tree[p, tile(t), :] = jnp.where(face_mask(2, SUB), news[t], spin(news[t + 4], 2))
         sweep(body, unroll=NP)
@@ -581,6 +601,8 @@
         products(k)
         for face in range(FACES):
             comm.wait_recv(rnd, face)
+            if face == 1:
+                x_terms(k, rnd)
         late_terms(k, rnd)
 
         @pl.when(k < CG_ITERS - 1)
@@ -745,8 +767,8 @@
         rounds, reds = 3, (2,)
         work = [vm(*field), vm(*field), vm(*field), vm(*block), vm(*block), vm(NP, ROWS, FACES, *TILE), vm(*block)]
     work += [vm(NP, FOLD, LANES), vm(LANES, LANES), vm(*block), vm(*block)]
-    sides = [vm(rounds, 2, FOLD, LANES), vm(rounds, 2, NP, 1, LANES)]
-    faces = sides + [vm(rounds, FOLD, LANES)] + sides + [vm(rounds, 2, FOLD, LANES)]
+    x_side, y_side = vm(rounds, 2, FOLD, LANES), vm(rounds + 1, 2, NP, 1, LANES)
+    faces = [x_side, y_side, vm(rounds, 2, NP, LANES)] * 2
     sizes = [counts[0], counts[1] * counts[2]]
     rows = [vm(*reds, 2, 1, LANES)] + [vm(*reds, n, 1, LANES) for n in sizes]
     dma = pltpu.SemaphoreType.DMA

time: 247 us -> 243 us (0.984)
  Pallas kernels: 244 us -> 241 us
where the time goes in v6:
time: 243 us
  Pallas kernels  241 us (99%)
    pallas_call x1, Pallas kernels, local_solve(): call(plain_kernel, 'plain', 1)(*args)  189 us
    pallas_call x1, Pallas kernels, local_solve(): call(basis_kernel, 'basis', 0, jax.ShapeDtypeStruct((1, 1), jnp.int32))  50.6 us

profile of v6, /device:TPU:0, one launch (start us, length us, event | category | flops | bytes accessed | tf_op | source)
XLA Modules:
  0.0 243.0 jit_solution(6882039913103898099)
XLA Ops:
  0.6 0.0 copy-start
  0.6 0.0 copy-start.1
  0.7 0.0 copy-start.2
  0.7 0.0 copy-start.3
  0.7 50.6 %basis.1 = (f32[32,64,64]{2,1,0:T(8,128)S(1)}, f32[32,64,64]{2,1,0:T(8,128)S(1)}, f32[1,128]{1,0:T(1,128)S(1)}, s32[1,1]{1,0:T(1,128)}) custom-call(f32[32,64,64]{2,1,0:T(8,128)} %k_hbm.1, f32[6,256,256]{2,1,0:T(8,128)} %g_hbm.1, f32[32,64,64]{2,1,0:T(8,128)} %f_hbm.1, f32[32,64,64]{2,1,0:T(8,128)} %u_hbm.1), custom_call_target="tpu_custom_call" | custom-call | tf_op jit(solution)/shard_map/basis/pallas_call | solution.py:799
  51.9 0.0 copy-done
  51.9 0.0 copy-done.1
  51.9 0.0 copy-done.2
  51.9 0.0 copy-done.3
  52.0 189.7 %conditional.1 = (f32[32,64,64]{2,1,0:T(8,128)S(1)}, f32[32,64,64]{2,1,0:T(8,128)S(1)}, f32[8]{0:T(128)S(1)}) conditional(s32[]{:T(128)} %bitcast.2, (f32[32,64,64]{2,1,0:T(8,128)S(1)}, f32[6,256,256]{2,1,0:T(8,128)S(1)}, f32[32,64,64]{2,1,0:T(8,128)S(1)}, f32[32,64,64]{2,1,0:T(8,128)S(1)}) %tuple.31, (f32[1,128]{1,0:T(1,128)S(1)}, ...), branch_computations={%region_0.0_spmd, %region_1.0_spmd} | conditional | bytes 88 | solution.py:800
  52.0 189.1 %plain.1 = (f32[32,64,64]{2,1,0:T(8,128)S(1)}, f32[32,64,64]{2,1,0:T(8,128)S(1)}, f32[1,128]{1,0:T(1,128)}) custom-call(f32[32,64,64]{2,1,0:T(8,128)S(1)} %get-tuple-element.21.k_hbm, f32[6,256,256]{2,1,0:T(8,128)S(1)} %get-tuple-element.22.g_hbm, f32[32,64,64]{2,1,0:T(8,128)S(1)} %get-tuple-element.23.f_hbm, f32[32,64,64]{2,1,0:T(8,128)S(1)} %get-tuple-element.24.u_hbm), custom_call_target="tpu_custom_call" | custom-call | tf_op jit(solution)/shard_map/cond/branch_0_fun/plain/pallas_call | solution.py:801
  241.0 0.6 slice_bitcast_fusion
  241.7 0.0 copy-start.4
  241.7 1.3 finish.1
  243.0 0.0 copy-done.4
Async XLA Ops:
  0.6 51.3 %copy-start = (f32[6,256,256]{2,1,0:T(8,128)S(1)}, f32[6,256,256]{2,1,0:T(8,128)}, u32[]{:S(2)}) copy-start(f32[6,256,256]{2,1,0:T(8,128)} %g_hbm.1) | copy-start | bytes 4718596
  0.6 51.3 %copy-start.1 = (f32[32,64,64]{2,1,0:T(8,128)S(1)}, f32[32,64,64]{2,1,0:T(8,128)}, u32[]{:S(2)}) copy-start(f32[32,64,64]{2,1,0:T(8,128)} %k_hbm.1) | copy-start | bytes 1572868
  0.7 51.3 %copy-start.2 = (f32[32,64,64]{2,1,0:T(8,128)S(1)}, f32[32,64,64]{2,1,0:T(8,128)}, u32[]{:S(2)}) copy-start(f32[32,64,64]{2,1,0:T(8,128)} %f_hbm.1) | copy-start | bytes 1572868
  0.7 51.3 %copy-start.3 = (f32[32,64,64]{2,1,0:T(8,128)S(1)}, f32[32,64,64]{2,1,0:T(8,128)}, u32[]{:S(2)}) copy-start(f32[32,64,64]{2,1,0:T(8,128)} %u_hbm.1) | copy-start | bytes 1572868
  241.7 1.3 copy-start.4

commit v7 on v6

--- a/solution.py
+++ b/solution.py
@@ -532,7 +532,7 @@
                 coef_ref[p, t, i] = scaled[i]
             z_ref[1, p + 1, own(t), :] = resid * inv
 
-    sweep(first, unroll=4)
+    sweep(first, unroll=8)
     send_faces(comm, 2, z_ref.at[1], tree)
 
     def products(k):
@@ -546,7 +546,7 @@
                     accs[i] = accs[i] + ddz * z_ref[i + 1, p + 1, own(t), :]
                 accs[NB] = accs[NB] + dz * z_k
                 accs[NB + 1] = accs[NB + 1] + dz * z_ref[k, p + 1, own(t), :]
-        accs = sweep(body, zero_tiles(NB + 2))
+        accs = sweep(body, zero_tiles(NB + 2), unroll=4)
         rows = [GRAM + NB * k + i for i in range(NB)] + [2 * k + 1, 2 * k]
         for row, acc in zip(rows, accs):
             sums_ref[pl.ds(row, 1), :] = row_sum(acc)
@@ -642,7 +642,7 @@
             r_out[p + NP, rows, :] = turn_half(rt)[:, :HALF]
         return carry
 
-    lax.fori_loop(0, NP, combine, 0, unroll=4)
+    lax.fori_loop(0, NP, combine, 0, unroll=8)
     h_ref[...] = squares_row(hist_ref, full_ref)
     ok_ref[0, 0] = ok[0, 0].astype(jnp.int32)
 

time: 243 us -> 243 us (level)
  no operation moved by 1% of the time
where the time goes in v7:
time: 243 us
  Pallas kernels  241 us (99%)
    pallas_call x1, Pallas kernels, local_solve(): call(plain_kernel, 'plain', 1)(*args)  189 us
    pallas_call x1, Pallas kernels, local_solve(): call(basis_kernel, 'basis', 0, jax.ShapeDtypeStruct((1, 1), jnp.int32))  50.4 us

profile of v7, /device:TPU:0, one launch (start us, length us, event | category | flops | bytes accessed | tf_op | source)
XLA Modules:
  0.0 242.8 jit_solution(6804844238457095730)
XLA Ops:
  0.6 0.0 copy-start
  0.6 0.0 copy-start.1
  0.7 0.0 copy-start.2
  0.7 0.0 copy-start.3
  0.7 50.4 %basis.1 = (f32[32,64,64]{2,1,0:T(8,128)S(1)}, f32[32,64,64]{2,1,0:T(8,128)S(1)}, f32[1,128]{1,0:T(1,128)S(1)}, s32[1,1]{1,0:T(1,128)}) custom-call(f32[32,64,64]{2,1,0:T(8,128)} %k_hbm.1, f32[6,256,256]{2,1,0:T(8,128)} %g_hbm.1, f32[32,64,64]{2,1,0:T(8,128)} %f_hbm.1, f32[32,64,64]{2,1,0:T(8,128)} %u_hbm.1), custom_call_target="tpu_custom_call" | custom-call | tf_op jit(solution)/shard_map/basis/pallas_call | solution.py:799
  51.7 0.0 copy-done
  51.7 0.0 copy-done.1
  51.7 0.0 copy-done.2
  51.7 0.0 copy-done.3
  51.7 189.7 %conditional.1 = (f32[32,64,64]{2,1,0:T(8,128)S(1)}, f32[32,64,64]{2,1,0:T(8,128)S(1)}, f32[8]{0:T(128)S(1)}) conditional(s32[]{:T(128)} %bitcast.2, (f32[32,64,64]{2,1,0:T(8,128)S(1)}, f32[6,256,256]{2,1,0:T(8,128)S(1)}, f32[32,64,64]{2,1,0:T(8,128)S(1)}, f32[32,64,64]{2,1,0:T(8,128)S(1)}) %tuple.31, (f32[1,128]{1,0:T(1,128)S(1)}, ...), branch_computations={%region_0.0_spmd, %region_1.0_spmd} | conditional | bytes 88 | solution.py:800
  51.7 189.1 %plain.1 = (f32[32,64,64]{2,1,0:T(8,128)S(1)}, f32[32,64,64]{2,1,0:T(8,128)S(1)}, f32[1,128]{1,0:T(1,128)}) custom-call(f32[32,64,64]{2,1,0:T(8,128)S(1)} %get-tuple-element.21.k_hbm, f32[6,256,256]{2,1,0:T(8,128)S(1)} %get-tuple-element.22.g_hbm, f32[32,64,64]{2,1,0:T(8,128)S(1)} %get-tuple-element.23.f_hbm, f32[32,64,64]{2,1,0:T(8,128)S(1)} %get-tuple-element.24.u_hbm), custom_call_target="tpu_custom_call" | custom-call | tf_op jit(solution)/shard_map/cond/branch_0_fun/plain/pallas_call | solution.py:801
  240.8 0.6 slice_bitcast_fusion
  241.5 0.0 copy-start.4
  241.5 1.3 finish.1
  242.8 0.0 copy-done.4
Async XLA Ops:
  0.6 51.1 %copy-start = (f32[6,256,256]{2,1,0:T(8,128)S(1)}, f32[6,256,256]{2,1,0:T(8,128)}, u32[]{:S(2)}) copy-start(f32[6,256,256]{2,1,0:T(8,128)} %g_hbm.1) | copy-start | bytes 4718596
  0.6 51.1 %copy-start.1 = (f32[32,64,64]{2,1,0:T(8,128)S(1)}, f32[32,64,64]{2,1,0:T(8,128)}, u32[]{:S(2)}) copy-start(f32[32,64,64]{2,1,0:T(8,128)} %k_hbm.1) | copy-start | bytes 1572868
  0.7 51.1 %copy-start.2 = (f32[32,64,64]{2,1,0:T(8,128)S(1)}, f32[32,64,64]{2,1,0:T(8,128)}, u32[]{:S(2)}) copy-start(f32[32,64,64]{2,1,0:T(8,128)} %f_hbm.1) | copy-start | bytes 1572868
  0.7 51.1 %copy-start.3 = (f32[32,64,64]{2,1,0:T(8,128)S(1)}, f32[32,64,64]{2,1,0:T(8,128)}, u32[]{:S(2)}) copy-start(f32[32,64,64]{2,1,0:T(8,128)} %u_hbm.1) | copy-start | bytes 1572868
  241.5 1.3 copy-start.4

commit v8 on v7

--- a/solution.py
+++ b/solution.py
@@ -23,6 +23,7 @@
 TILE = (SUB, LANES)
 WIDE = (2 * SUB, LANES)
 FACES = 6
+PARTS = 4
 FOLD = NY // 2
 TURNS = ((4, 8, 12), (16, 32, 48))
 
@@ -365,6 +366,21 @@
             lax.fori_loop(1, rounds, clear, 0)
 
 
+class Parts:
+    def __init__(self, src, dst, sems, first):
+        step = NX // PARTS
+        self.copies = [pltpu.make_async_copy(src.at[pl.ds(step * i, step)], dst.at[pl.ds(step * i, step)],
+                                             sems.at[first + i]) for i in range(PARTS)]
+
+    def start(self):
+        for copy in self.copies:
+            copy.start()
+
+    def wait(self):
+        for copy in self.copies:
+            copy.wait()
+
+
 def lanes_of(pos):
     return pl.ds(pl.multiple_of(lax.div(pos, 2) * LANES, LANES), LANES)
 
@@ -372,8 +388,8 @@
 def start_up(comm, ins, raws, slabs, load_sem):
     k_hbm, g_hbm, f_hbm, u_hbm = ins
     px, py, pz = comm.pos
-    loads = [pltpu.make_async_copy(k_hbm, raws[0], load_sem.at[0]),
-             pltpu.make_async_copy(u_hbm, raws[1], load_sem.at[1])]
+    loads = [Parts(k_hbm, raws[0], load_sem, FACES),
+             Parts(u_hbm, raws[1], load_sem, FACES + PARTS)]
     x_row = jnp.where(comm.has[1], 0, 1)
     y_row = jnp.where(comm.has[3], 2, 3)
     z_row = jnp.where(comm.has[5], 4, 5)
@@ -385,7 +401,7 @@
         g_hbm.at[y_row, pl.ds(pl.multiple_of(px * NX, NX), NX), z_lanes], slabs[1], load_sem.at[3]))
     loads.append(pltpu.make_async_copy(
         g_hbm.at[z_row, pl.ds(pl.multiple_of(px * NX, NX), NX), y_lanes], slabs[2], load_sem.at[4]))
-    loads.append(pltpu.make_async_copy(f_hbm, raws[2], load_sem.at[5]))
+    loads.append(Parts(f_hbm, raws[2], load_sem, FACES + 2 * PARTS))
     for load in loads:
         load.start()
     return loads
@@ -747,7 +763,7 @@
 
 
 def finish_kernel(u_in, r_in, u_hbm, r_hbm, sems):
-    copies = [pltpu.make_async_copy(u_in, u_hbm, sems.at[0]), pltpu.make_async_copy(r_in, r_hbm, sems.at[1])]
+    copies = [Parts(u_in, u_hbm, sems, 0), Parts(r_in, r_hbm, sems, PARTS)]
     for copy in copies:
         copy.start()
     for copy in copies:
@@ -772,7 +788,7 @@
     sizes = [counts[0], counts[1] * counts[2]]
     rows = [vm(*reds, 2, 1, LANES)] + [vm(*reds, n, 1, LANES) for n in sizes]
     dma = pltpu.SemaphoreType.DMA
-    sems = [dma((6,)), dma((rounds, 6)), dma((rounds, 6)), dma((*reds, 2, max(sizes))), dma((*reds, 2, max(sizes)))]
+    sems = [dma((FACES + 3 * PARTS,)), dma((rounds, 6)), dma((rounds, 6)), dma((*reds, 2, max(sizes))), dma((*reds, 2, max(sizes)))]
     return raws + work + faces + rows + sems
 
 
@@ -804,7 +820,7 @@
             out_shape=(block, block),
             in_specs=[pl.BlockSpec(memory_space=pltpu.VMEM)] * 2,
             out_specs=(pl.BlockSpec(memory_space=pltpu.HBM),) * 2,
-            scratch_shapes=[pltpu.SemaphoreType.DMA((2,))],
+            scratch_shapes=[pltpu.SemaphoreType.DMA((2 * PARTS,))],
             compiler_params=pltpu.CompilerParams(vmem_limit_bytes=VMEM_BYTES),
             name='finish',
         )(u_out, r_out)

time: 243 us -> 243 us (level)
  no operation moved by 1% of the time
where the time goes in v8:
time: 243 us
  Pallas kernels  241 us (99%)
    pallas_call x1, Pallas kernels, local_solve(): call(plain_kernel, 'plain', 1)(*args)  189 us
    pallas_call x1, Pallas kernels, local_solve(): call(basis_kernel, 'basis', 0, jax.ShapeDtypeStruct((1, 1), jnp.int32))  50.5 us

profile of v8, /device:TPU:0, one launch (start us, length us, event | category | flops | bytes accessed | tf_op | source)
XLA Modules:
  0.0 243.1 jit_solution(760182401138329457)
XLA Ops:
  0.6 0.0 copy-start
  0.6 0.0 copy-start.1
  0.7 0.0 copy-start.2
  0.7 0.0 copy-start.3
  0.7 50.5 %basis.1 = (f32[32,64,64]{2,1,0:T(8,128)S(1)}, f32[32,64,64]{2,1,0:T(8,128)S(1)}, f32[1,128]{1,0:T(1,128)S(1)}, s32[1,1]{1,0:T(1,128)}) custom-call(f32[32,64,64]{2,1,0:T(8,128)} %k_hbm.1, f32[6,256,256]{2,1,0:T(8,128)} %g_hbm.1, f32[32,64,64]{2,1,0:T(8,128)} %f_hbm.1, f32[32,64,64]{2,1,0:T(8,128)} %u_hbm.1), custom_call_target="tpu_custom_call" | custom-call | tf_op jit(solution)/shard_map/basis/pallas_call | solution.py:815
  51.8 0.0 copy-done
  51.8 0.0 copy-done.1
  51.8 0.0 copy-done.2
  51.8 0.0 copy-done.3
  51.8 189.8 %conditional.1 = (f32[32,64,64]{2,1,0:T(8,128)S(1)}, f32[32,64,64]{2,1,0:T(8,128)S(1)}, f32[8]{0:T(128)S(1)}) conditional(s32[]{:T(128)} %bitcast.2, (f32[32,64,64]{2,1,0:T(8,128)S(1)}, f32[6,256,256]{2,1,0:T(8,128)S(1)}, f32[32,64,64]{2,1,0:T(8,128)S(1)}, f32[32,64,64]{2,1,0:T(8,128)S(1)}) %tuple.31, (f32[1,128]{1,0:T(1,128)S(1)}, ...), branch_computations={%region_0.0_spmd, %region_1.0_spmd} | conditional | bytes 88 | solution.py:816
  51.8 189.2 %plain.1 = (f32[32,64,64]{2,1,0:T(8,128)S(1)}, f32[32,64,64]{2,1,0:T(8,128)S(1)}, f32[1,128]{1,0:T(1,128)}) custom-call(f32[32,64,64]{2,1,0:T(8,128)S(1)} %get-tuple-element.21.k_hbm, f32[6,256,256]{2,1,0:T(8,128)S(1)} %get-tuple-element.22.g_hbm, f32[32,64,64]{2,1,0:T(8,128)S(1)} %get-tuple-element.23.f_hbm, f32[32,64,64]{2,1,0:T(8,128)S(1)} %get-tuple-element.24.u_hbm), custom_call_target="tpu_custom_call" | custom-call | tf_op jit(solution)/shard_map/cond/branch_0_fun/plain/pallas_call | solution.py:817
  241.0 0.6 slice_bitcast_fusion
  241.6 0.0 copy-start.4
  241.7 1.4 finish.1
  243.1 0.0 copy-done.4
Async XLA Ops:
  0.6 51.1 %copy-start = (f32[6,256,256]{2,1,0:T(8,128)S(1)}, f32[6,256,256]{2,1,0:T(8,128)}, u32[]{:S(2)}) copy-start(f32[6,256,256]{2,1,0:T(8,128)} %g_hbm.1) | copy-start | bytes 4718596
  0.6 51.1 %copy-start.1 = (f32[32,64,64]{2,1,0:T(8,128)S(1)}, f32[32,64,64]{2,1,0:T(8,128)}, u32[]{:S(2)}) copy-start(f32[32,64,64]{2,1,0:T(8,128)} %k_hbm.1) | copy-start | bytes 1572868
  0.7 51.1 %copy-start.2 = (f32[32,64,64]{2,1,0:T(8,128)S(1)}, f32[32,64,64]{2,1,0:T(8,128)}, u32[]{:S(2)}) copy-start(f32[32,64,64]{2,1,0:T(8,128)} %f_hbm.1) | copy-start | bytes 1572868
  0.7 51.1 %copy-start.3 = (f32[32,64,64]{2,1,0:T(8,128)S(1)}, f32[32,64,64]{2,1,0:T(8,128)}, u32[]{:S(2)}) copy-start(f32[32,64,64]{2,1,0:T(8,128)} %u_hbm.1) | copy-start | bytes 1572868
  241.6 1.4 copy-start.4
